TPU v7x, 256 devices: a whole 4x4x8 slice. The times are simulated.
256 devices in a mesh: rows: 32 (over y, x, core), grp: 8 (over z).
Axes of the slice: x: 4, y: 4, z: 8, core: 2. Of those that a mesh axis runs over, the one named last changes fastest.
Arguments:
- matrix: bfloat16 [131072, 2048], P(('rows', 'grp')), may hold values from -0.0625 to 0.0625
- right_side: bfloat16 [131072, 128], P(('rows', 'grp')), may hold values from -6 to 6
- precond: bfloat16 [2048, 2048], replicated, may hold values from -1 to 3
- row_counts: int32 [256], P(('rows', 'grp')), may hold values from 64 to 512, as said below
Outputs:
- solution: float32 [2048, 128], P(None, 'grp')
- coeffs: float32 [2048, 128], P(None, 'grp')
- rel_residual: float32 [128], P('grp')
Inputs may be any that keep to these rules, and one draw needn't show every extreme that they name: Device d holds A's rows in its first row_counts[d] slots of 512; some device is full in every draw.
All inputs are finite; a program needn't handle non-finite values.
Results may differ from a plain program's by a relative error of at most 0.0128.
Values may be sent and summed in bfloat16 or wider, within the bound.
A program may use at most 64 MiB of HBM per device.

v0:
```python
import jax
import jax.numpy as jnp
from jax import lax
from jax.sharding import PartitionSpec as P

ITERS = 3


floor_sq = 0.01


def cut_along(value, dim, peers):
    lengths = value.shape
    tiles = value.reshape(*lengths[:dim], peers, lengths[dim] // peers, *lengths[dim + 1 :])
    return jnp.moveaxis(tiles, dim, 0)


def sent_and_summed(value, axis, dim):
    peers = lax.axis_size(axis)
    tiles = lax.all_to_all(cut_along(value, dim, peers), axis, 0, 0, tiled=True)
    return jnp.sum(tiles, axis=0)


def sent_together(arrays, axis, dim, along):
    both = jnp.concatenate(arrays, axis=along)
    filled, at, gathered = (sent_and_summed(both, axis, dim), 0, [])
    for a in arrays:
        gathered.append(lax.slice_in_dim(filled, at, at + a.shape[along], axis=along))
        at += a.shape[along]
    return tuple(gathered)


def rows_for(lines, peers):
    spare = -lines.shape[0] % peers
    if not spare:
        return lines
    return jnp.concatenate([lines, jnp.zeros((spare, *lines.shape[1:]), lines.dtype)])


def joined_along(tiles, dim):
    lengths = list(tiles.shape[1:])
    lengths[dim] *= tiles.shape[0]
    return jnp.moveaxis(tiles, 0, dim).reshape(lengths)


def copy_for_each(value, axis):
    copies = jnp.broadcast_to(value, (lax.axis_size(axis), *value.shape))
    return lax.all_to_all(copies, axis, split_axis=0, concat_axis=0, tiled=True)


def gathered_copies(value, axis, dim):
    return joined_along(copy_for_each(value, axis), dim)


def sum_by_parts(value, axes):
    own = sent_and_summed(rows_for(value, lax.axis_size(axes)), axes, 0)
    whole = gathered_copies(own, axes, 0)
    return whole[: len(value)].reshape(value.shape)


def in_one(arrays, axis):
    ravelled, at, gathered = (jnp.concatenate([a.reshape(-1) for a in arrays]), 0, [])
    subtotal = sum_by_parts(ravelled, axis)
    for a in arrays:
        gathered.append(subtotal[at : at + a.size].reshape(a.shape))
        at += a.size
    return tuple(gathered)


def pull_partial(matrix, residue):
    partial_value = lax.dot_general(
        matrix,
        residue.astype(jnp.bfloat16),
        (((0,), (0,)), ((), ())),
        preferred_element_type=jnp.float32,
    )
    squares = jnp.sum(residue * residue, axis=0, keepdims=True)
    return (partial_value, squares)


def column_section(precond, partial_value, squares, right_vec):
    u_norm = jnp.sqrt(squares + floor_sq)
    pulled = lax.dot_general(
        precond,
        (partial_value / u_norm).astype(jnp.bfloat16),
        (((0,), (0,)), ((), ())),
        preferred_element_type=jnp.float32,
    )
    raw_vec = pulled - u_norm * right_vec
    v_norm = jnp.sqrt(jnp.sum(raw_vec * raw_vec, axis=0, keepdims=True) + floor_sq)
    return (u_norm, raw_vec / v_norm, v_norm)


def shards(matrix, right_side, precond, row_counts):
    local_rows, width = matrix.shape
    count = row_counts[0]
    live_rows = (lax.broadcasted_iota(jnp.int32, (local_rows, 1), 0) < count).astype(jnp.float32)

    def row_pass(pushed, v_norm_all, left_vec):
        if pushed is None:
            residue = live_rows * right_side.astype(jnp.float32)
        else:
            residue = live_rows * (
                jnp.dot(matrix, pushed, preferred_element_type=jnp.float32) - v_norm_all * left_vec
            )
        partial_value, squares = pull_partial(matrix, residue)
        return (residue, partial_value, squares)

    def reduce_cols(partial_value, squares):
        shared, shared_sq = sent_together((partial_value, squares), "grp", 1, 0)
        return in_one((shared, shared_sq), "rows")

    def share_cols(right_vec, v_norm, u_norm):
        pushed = jnp.dot(
            precond, right_vec.astype(jnp.bfloat16), preferred_element_type=jnp.float32
        ).astype(jnp.bfloat16)
        pushed = gathered_copies(pushed, "grp", 1)
        norms = gathered_copies(jnp.concatenate([v_norm, u_norm], axis=0), "grp", 1)
        return (pushed, norms[0:1], norms[1:2])

    residue, partial_value, squares = row_pass(None, None, None)
    partial_value, squares = reduce_cols(partial_value, squares)
    u_norm, right_vec, v_norm = column_section(
        precond, partial_value, squares, jnp.zeros((width, partial_value.shape[1]), jnp.float32)
    )
    phi_bar = u_norm
    rho_bar = v_norm
    search = right_vec
    coeffs = jnp.zeros(right_vec.shape, jnp.float32)
    start_norm = u_norm
    pushed, v_norm_all, u_norm_all = share_cols(right_vec, v_norm, u_norm)
    left_vec = residue / u_norm_all
    for turn_index in range(ITERS):
        residue, partial_value, squares = row_pass(pushed, v_norm_all, left_vec)
        partial_value, squares = reduce_cols(partial_value, squares)
        u_norm, next_vec, next_norm = column_section(precond, partial_value, squares, right_vec)
        radius = jnp.sqrt(rho_bar * rho_bar + u_norm * u_norm)
        cosine = rho_bar / radius
        sine_part = u_norm / radius
        coupling = sine_part * next_norm
        rho_bar = -cosine * next_norm
        phi_step = cosine * phi_bar
        phi_bar = sine_part * phi_bar
        coeffs = coeffs + phi_step / radius * search
        search = next_vec - coupling / radius * search
        right_vec = next_vec
        v_norm = next_norm
        if turn_index + 1 < ITERS:
            pushed, v_norm_all, u_norm_all = share_cols(right_vec, v_norm, u_norm)
            left_vec = residue / u_norm_all
    ratio = phi_bar / start_norm
    solution = jnp.dot(precond, coeffs.astype(jnp.bfloat16), preferred_element_type=jnp.float32)
    return (solution, coeffs, ratio[0])


def solution(mesh):
    return jax.shard_map(
        shards,
        mesh=mesh,
        in_specs=(P(("rows", "grp"), None), P(("rows", "grp"), None), P(), P(("rows", "grp"))),
        out_specs=(P(None, "grp"), P(None, "grp"), P("grp")),
        check_vma=False,
    )
```

profile of v0, /device:TPU:1, one launch (start us, length us, event | category | flops | bytes accessed | tf_op | source)
XLA Modules:
  0.0 400.8 jit_solution(16813123153177191530)
XLA Ops:
  3.3 37.6 %all_to_all.110 = f32[8,2049,16]{1,2,0:T(8,128)S(1)} all-to-all(f32[8,2049,16]{1,2,0:T(8,128)S(1)} %maximum_bitcast_fusion), channel_id=1, replica_groups=mesh['rows'=32,'grp'=8] {'grp'}, dimensions={0} | all-to-all | bytes 2098176 | tf_op jit(solution)/shard_map/all_to_all | solution.py:20
  44.4 16.9 %all_to_all.111 = f32[32,1,1025]{2,1,0:T(1,128)S(1)} all-to-all(f32[32,1,1025]{2,1,0:T(1,128)S(1)} %all_to_all.71), channel_id=1, replica_groups=mesh['rows'=32,'grp'=8] {'rows'}, dimensions={0} | all-to-all | bytes 262400 | tf_op jit(solution)/shard_map/all_to_all | solution.py:20
  61.5 11.4 %all_to_all.112 = f32[32,1,1025]{2,1,0:T(1,128)S(1)} all-to-all(f32[32,1,1025]{2,1,0:T(1,128)S(1)} %broadcast_in_dim.38), channel_id=1, replica_groups=mesh['rows'=32,'grp'=8] {'rows'}, dimensions={0} | all-to-all | bytes 262400 | tf_op jit(solution)/shard_map/all_to_all | solution.py:48
  84.1 5.7 %fusion = bf16[2048,16]{0,1:T(8,128)(2,1)S(1)} fusion(bf16[2048,2048]{1,0:T(8,128)(2,1)} %param.6, f32[16,2048]{1,0:T(8,128)S(1)} %get-tuple-element.34, f32[16]{0:T(128)S(1)} %get-tuple-element.32), kind=kOutput, calls=%fused_computation.7 | convolution fusion | flops 134316032 | bytes 8585280 | tf_op jit(solution)/shard_map/dot_general | solution.py:114
  91.4 5.7 %all-to-all-start.3 = ((bf16[8,2048,16]{1,2,0:T(8,128)(2,1)}), bf16[8,2048,16]{1,2,0:T(8,128)(2,1)S(1)}, u32[]{:S(2)}, u32[]{:S(2)}) async-start(bf16[8,2048,16]{1,2,0:T(8,128)(2,1)} %broadcast_in_dim.39), calls=%async_computation.3 | async-start | bytes 1048576 | tf_op jit(solution)/shard_map/all_to_all | solution.py:48
  97.3 17.8 %all-to-all-done.3 = bf16[8,2048,16]{1,2,0:T(8,128)(2,1)S(1)} async-done(((bf16[8,2048,16]{1,2,0:T(8,128)(2,1)}), bf16[8,2048,16]{1,2,0:T(8,128)(2,1)S(1)}, u32[]{:S(2)}, u32[]{:S(2)}) %all-to-all-start.3) | async-done | bytes 524320 | tf_op jit(solution)/shard_map/all_to_all | solution.py:48
  116.8 32.3 %all_to_all.113 = f32[8,2049,16]{1,2,0:T(8,128)S(1)} all-to-all(f32[8,2049,16]{1,2,0:T(8,128)S(1)} %maximum_bitcast_fusion.1), channel_id=1, replica_groups=mesh['rows'=32,'grp'=8] {'grp'}, dimensions={0} | all-to-all | bytes 2098176 | tf_op jit(solution)/shard_map/all_to_all | solution.py:20
  151.8 12.1 %all_to_all.114 = f32[32,1,1025]{2,1,0:T(1,128)S(1)} all-to-all(f32[32,1,1025]{2,1,0:T(1,128)S(1)} %all_to_all.77), channel_id=1, replica_groups=mesh['rows'=32,'grp'=8] {'rows'}, dimensions={0} | all-to-all | bytes 262400 | tf_op jit(solution)/shard_map/all_to_all | solution.py:20
  164.1 11.4 %all_to_all.115 = f32[32,1,1025]{2,1,0:T(1,128)S(1)} all-to-all(f32[32,1,1025]{2,1,0:T(1,128)S(1)} %broadcast_in_dim.41), channel_id=1, replica_groups=mesh['rows'=32,'grp'=8] {'rows'}, dimensions={0} | all-to-all | bytes 262400 | tf_op jit(solution)/shard_map/all_to_all | solution.py:48
  178.0 4.7 %multiply_reduce_fusion.5 = (f32[16]{0:T(128)S(1)}, f32[16,2048]{1,0:T(8,128)S(1)}) fusion(f32[16,2048]{1,0:T(8,128)S(1)} %get-tuple-element.34, f32[16]{0:T(128)S(1)} %get-tuple-element.32, f32[16]{0:T(128)S(1)} %get-tuple-element.21, bf16[2048,2048]{1,0:T(8,128)(2,1)} %param.6, f32[2050,16]{1,0:T(8,128)S(1)} %slice.99), kind=kOutput, calls=%fused_computation.41 | convolution fusion | flops 134447088 | bytes 9700928 | tf_op jit(solution)/shard_map/dot_general | solution.py:83
  186.7 5.7 %fusion.1 = bf16[2048,16]{0,1:T(8,128)(2,1)S(1)} fusion(bf16[2048,2048]{1,0:T(8,128)(2,1)} %param.6, f32[16,2048]{1,0:T(8,128)S(1)} %get-tuple-element.38, f32[16]{0:T(128)S(1)} %get-tuple-element.30), kind=kOutput, calls=%fused_computation.8 | convolution fusion | flops 134316032 | bytes 8585280 | tf_op jit(solution)/shard_map/dot_general | solution.py:114
  194.0 5.8 %all-to-all-start.8 = ((bf16[8,2048,16]{1,2,0:T(8,128)(2,1)}), bf16[8,2048,16]{1,2,0:T(8,128)(2,1)S(1)}, u32[]{:S(2)}, u32[]{:S(2)}) async-start(bf16[8,2048,16]{1,2,0:T(8,128)(2,1)} %broadcast_in_dim.42), calls=%async_computation.8 | async-start | bytes 1048576 | tf_op jit(solution)/shard_map/all_to_all | solution.py:48
  200.0 17.8 %all-to-all-done.8 = bf16[8,2048,16]{1,2,0:T(8,128)(2,1)S(1)} async-done(((bf16[8,2048,16]{1,2,0:T(8,128)(2,1)}), bf16[8,2048,16]{1,2,0:T(8,128)(2,1)S(1)}, u32[]{:S(2)}, u32[]{:S(2)}) %all-to-all-start.8) | async-done | bytes 524320 | tf_op jit(solution)/shard_map/all_to_all | solution.py:48
  219.5 32.0 %all_to_all.116 = f32[8,2049,16]{1,2,0:T(8,128)S(1)} all-to-all(f32[8,2049,16]{1,2,0:T(8,128)S(1)} %maximum_bitcast_fusion.2), channel_id=1, replica_groups=mesh['rows'=32,'grp'=8] {'grp'}, dimensions={0} | all-to-all | bytes 2098176 | tf_op jit(solution)/shard_map/all_to_all | solution.py:20
  258.0 12.3 %all_to_all.117 = f32[32,1,1025]{2,1,0:T(1,128)S(1)} all-to-all(f32[32,1,1025]{2,1,0:T(1,128)S(1)} %all_to_all.83), channel_id=1, replica_groups=mesh['rows'=32,'grp'=8] {'rows'}, dimensions={0} | all-to-all | bytes 262400 | tf_op jit(solution)/shard_map/all_to_all | solution.py:20
  270.5 11.4 %all_to_all.118 = f32[32,1,1025]{2,1,0:T(1,128)S(1)} all-to-all(f32[32,1,1025]{2,1,0:T(1,128)S(1)} %broadcast_in_dim.44), channel_id=1, replica_groups=mesh['rows'=32,'grp'=8] {'rows'}, dimensions={0} | all-to-all | bytes 262400 | tf_op jit(solution)/shard_map/all_to_all | solution.py:48
  287.0 5.4 %multiply_reduce_fusion.4 = (f32[16]{0:T(128)S(1)}, f32[16,2048]{1,0:T(8,128)}) fusion(f32[16,2048]{1,0:T(8,128)S(1)} %get-tuple-element.38, f32[16]{0:T(128)S(1)} %get-tuple-element.30, f32[16]{0:T(128)S(1)} %get-tuple-element.19, bf16[2048,2048]{1,0:T(8,128)(2,1)} %param.6, f32[2050,16]{1,0:T(8,128)S(1)} %slice.106), kind=kOutput, calls=%fused_computation.40 | convolution fusion | flops 134447088 | bytes 9700928 | tf_op jit(solution)/shard_map/dot_general | solution.py:83
  296.3 5.8 %fusion.2 = bf16[2048,16]{0,1:T(8,128)(2,1)S(1)} fusion(bf16[2048,2048]{1,0:T(8,128)(2,1)} %param.6, f32[16,2048]{1,0:T(8,128)} %get-tuple-element.42, f32[16]{0:T(128)S(1)} %get-tuple-element.28), kind=kOutput, calls=%fused_computation.9 | convolution fusion | flops 134316032 | bytes 8585280 | tf_op jit(solution)/shard_map/dot_general | solution.py:114
  303.7 5.8 %all-to-all-start.13 = ((bf16[8,2048,16]{1,2,0:T(8,128)(2,1)}), bf16[8,2048,16]{1,2,0:T(8,128)(2,1)S(1)}, u32[]{:S(2)}, u32[]{:S(2)}) async-start(bf16[8,2048,16]{1,2,0:T(8,128)(2,1)} %broadcast_in_dim.45), calls=%async_computation.13 | async-start | bytes 1048576 | tf_op jit(solution)/shard_map/all_to_all | solution.py:48
  309.7 17.8 %all-to-all-done.13 = bf16[8,2048,16]{1,2,0:T(8,128)(2,1)S(1)} async-done(((bf16[8,2048,16]{1,2,0:T(8,128)(2,1)}), bf16[8,2048,16]{1,2,0:T(8,128)(2,1)S(1)}, u32[]{:S(2)}, u32[]{:S(2)}) %all-to-all-start.13) | async-done | bytes 524320 | tf_op jit(solution)/shard_map/all_to_all | solution.py:48
  329.2 32.0 %all_to_all.119 = f32[8,2049,16]{1,2,0:T(8,128)S(1)} all-to-all(f32[8,2049,16]{1,2,0:T(8,128)S(1)} %maximum_bitcast_fusion.3), channel_id=1, replica_groups=mesh['rows'=32,'grp'=8] {'grp'}, dimensions={0} | all-to-all | bytes 2098176 | tf_op jit(solution)/shard_map/all_to_all | solution.py:20
  367.7 12.3 %all_to_all.120 = f32[32,1,1025]{2,1,0:T(1,128)S(1)} all-to-all(f32[32,1,1025]{2,1,0:T(1,128)S(1)} %all_to_all.89), channel_id=1, replica_groups=mesh['rows'=32,'grp'=8] {'rows'}, dimensions={0} | all-to-all | bytes 262400 | tf_op jit(solution)/shard_map/all_to_all | solution.py:20
  380.2 11.4 %all_to_all.121 = f32[32,1,1025]{2,1,0:T(1,128)S(1)} all-to-all(f32[32,1,1025]{2,1,0:T(1,128)S(1)} %broadcast_in_dim.47), channel_id=1, replica_groups=mesh['rows'=32,'grp'=8] {'rows'}, dimensions={0} | all-to-all | bytes 262400 | tf_op jit(solution)/shard_map/all_to_all | solution.py:48
  394.5 6.4 %convolution_bitcast_fusion = f32[2048,16]{0,1:T(8,128)} fusion(bf16[2048,2048]{1,0:T(8,128)(2,1)} %param.6, f32[2048,16]{0,1:T(8,128)S(1)} %add_bitcast_fusion), kind=kOutput, calls=%fused_computation | convolution fusion | flops 134250496 | bytes 8650752 | tf_op jit(solution)/shard_map/dot_general | solution.py:152
  (112 shorter events, 61.6 us)
Async XLA Ops:
  0.6 2.2 copy-start
  80.7 9.9 %all-to-all-start.4 = ((f32[8,2,16]{2,1,0:T(2,128)}), f32[8,2,16]{2,1,0:T(2,128)S(1)}, u32[]{:S(2)}, u32[]{:S(2)}) async-start(f32[8,2,16]{2,1,0:T(2,128)} %broadcast_in_dim.40), calls=%async_computation.4 | async-start | bytes 16384 | tf_op jit(solution)/shard_map/all_to_all | solution.py:48
  91.4 23.7 %all-to-all-start.3 = ((bf16[8,2048,16]{1,2,0:T(8,128)(2,1)}), bf16[8,2048,16]{1,2,0:T(8,128)(2,1)S(1)}, u32[]{:S(2)}, u32[]{:S(2)}) async-start(bf16[8,2048,16]{1,2,0:T(8,128)(2,1)} %broadcast_in_dim.39), calls=%async_computation.3 | async-start | bytes 1048576 | tf_op jit(solution)/shard_map/all_to_all | solution.py:48
  116.0 0.7 copy-start.4
  183.3 9.9 %all-to-all-start.9 = ((f32[8,2,16]{2,1,0:T(2,128)}), f32[8,2,16]{2,1,0:T(2,128)S(1)}, u32[]{:S(2)}, u32[]{:S(2)}) async-start(f32[8,2,16]{2,1,0:T(2,128)} %broadcast_in_dim.43), calls=%async_computation.9 | async-start | bytes 16384 | tf_op jit(solution)/shard_map/all_to_all | solution.py:48
  186.7 31.1 %copy-start.5 = (f32[512,128]{0,1:T(8,128)S(1)}, f32[512,128]{0,1:T(8,128)}, u32[]{:S(2)}) copy-start(f32[512,128]{0,1:T(8,128)} %copy-done.4) | copy-start | bytes 786436
  194.0 23.7 %all-to-all-start.8 = ((bf16[8,2048,16]{1,2,0:T(8,128)(2,1)}), bf16[8,2048,16]{1,2,0:T(8,128)(2,1)S(1)}, u32[]{:S(2)}, u32[]{:S(2)}) async-start(bf16[8,2048,16]{1,2,0:T(8,128)(2,1)} %broadcast_in_dim.42), calls=%async_computation.8 | async-start | bytes 1048576 | tf_op jit(solution)/shard_map/all_to_all | solution.py:48
  218.7 0.7 copy-start.2
  293.0 9.9 %all-to-all-start.14 = ((f32[8,2,16]{2,1,0:T(2,128)}), f32[8,2,16]{2,1,0:T(2,128)S(1)}, u32[]{:S(2)}, u32[]{:S(2)}) async-start(f32[8,2,16]{2,1,0:T(2,128)} %broadcast_in_dim.46), calls=%async_computation.14 | async-start | bytes 16384 | tf_op jit(solution)/shard_map/all_to_all | solution.py:48
  296.3 31.2 %copy-start.3 = (f32[512,128]{0,1:T(8,128)S(1)}, f32[512,128]{0,1:T(8,128)}, u32[]{:S(2)}) copy-start(f32[512,128]{0,1:T(8,128)} %copy-done.2) | copy-start | bytes 786436
  303.7 23.8 %all-to-all-start.13 = ((bf16[8,2048,16]{1,2,0:T(8,128)(2,1)}), bf16[8,2048,16]{1,2,0:T(8,128)(2,1)S(1)}, u32[]{:S(2)}, u32[]{:S(2)}) async-start(bf16[8,2048,16]{1,2,0:T(8,128)(2,1)} %broadcast_in_dim.45), calls=%async_computation.13 | async-start | bytes 1048576 | tf_op jit(solution)/shard_map/all_to_all | solution.py:48
  394.5 6.4 %copy-start.1 = (f32[2048,16]{0,1:T(8,128)}, f32[2048,16]{0,1:T(8,128)S(1)}, u32[]{:S(2)}) copy-start(f32[2048,16]{0,1:T(8,128)S(1)} %add_bitcast_fusion) | copy-start | bytes 393220
where the time goes:
time: 402 us; the launch traced here: 401 us
  blocking collectives  233 us (58%)
  waiting for transfers between devices  55.7 us (14%)
  matrix products  42.8 us (11%)
  local copies, waits for them, and re-layouts  30.4 us (8%)
  starting transfers between devices  27.3 us (7%)
  other arithmetic  9.51 us (2%)
    all_to_all x8, blocking collectives, sent_and_summed(): tiles = lax.all_to_all(cut_along(value, dim, peers), axis, 0, 0, tiled=True)  188 us
    all_to_all x6, waiting for transfers between devices, copy_for_each(): return lax.all_to_all(copies, axis, split_axis=0, concat_axis=0, tiled=True)  55.7 us
    all_to_all x4, blocking collectives, copy_for_each(): return lax.all_to_all(copies, axis, split_axis=0, concat_axis=0, tiled=True)  45.6 us
    all_to_all x6, starting transfers between devices, copy_for_each(): return lax.all_to_all(copies, axis, split_axis=0, concat_axis=0, tiled=True)  27.3 us
    dot_general x3, matrix products, share_cols(): jnp.dot(precond, right_vec.astype(jnp.bfloat16), preferred_element_type=j...  17.1 us
    dot_general x3, matrix products, column_section(): lax.dot_general(precond, (partial_value / u_norm).astype(jnp.bfloat16), (...  14.8 us
    slice x12, local copies, waits for them, and re-layouts, sent_together(): lax.slice_in_dim(filled, at, at + a.shape[along], axis=along)  11.3 us
  transfers between devices with their start and end apart: 6, of which 6 were waited for; matrix products, arithmetic and copies ran while one was open for 4% of the time, Pallas kernels for 0%

commit v1 on v0

v1 whole, which is shorter than its diff:
```python
import functools

import jax
import jax.numpy as jnp
from jax import lax
from jax.experimental import pallas as pl
from jax.experimental.pallas import tpu as pltpu
from jax.sharding import PartitionSpec as P

ITERS = 3
FLOOR_SQ = 0.01
MESH = pl.DeviceIdType.MESH
SIDE = 4
CHIPS = SIDE * SIDE
LANES = 128
TILE = 256

NT = (((1,), (1,)), ((), ()))


def dot(a, b):
    return jnp.dot(a, b, preferred_element_type=jnp.float32)


def dot_nt(a, b):
    return lax.dot_general(a, b, NT, preferred_element_type=jnp.float32)


def reach(step):
    return min(step, SIDE - step)


OFFSETS = sorted(
    ((dy, dx) for dy in range(SIDE) for dx in range(SIDE) if dy or dx),
    key=lambda o: -(reach(o[0]) + reach(o[1])),
)


def wide(column, count):
    return jnp.concatenate([column] * count, axis=1)


def kernel(
    planes,
    count_ref, a_hbm, b_hbm, n_hbm,
    sol_ref, coef_ref, ratio_ref,
    a, b, n, rv, vb, pushed, pref, pb, q, part, partb, crecv, xsend, xrecv, zbuf,
    csq, xsq, zsq, search, coeffs, rho, phi, start, ucol, vcol,
    load_sem, cs_sem, cr_sem, xs_sem, xr_sem, zs_sem, zr_sem, gs_sem, gr_sem, fs_sem, fr_sem,
    csqs_sem, csqr_sem, xsqs_sem, xsqr_sem, zsqs_sem, zsqr_sem,
):
    columns, width = rv.shape
    rows = a.shape[0]
    half = columns // 2
    own_cols = columns // planes
    tiles = width // TILE
    per_tile = TILE // LANES

    r = lax.axis_index("rows")
    z = lax.axis_index("grp")
    core = lax.rem(r, 2)
    chip = lax.div(r, 2)
    x = lax.rem(chip, SIDE)
    y = lax.div(chip, SIDE)

    def chip_at(dy, dx):
        return lax.rem(y + dy, SIDE) * SIDE + lax.rem(x + dx, SIDE)

    plane_chips = [chip_at(dy, dx) for dy, dx in OFFSETS]
    other_planes = [lax.rem(z + k, planes) for k in sorted(range(1, planes), key=lambda k: -min(k, planes - k))]
    partner = {"rows": chip * 2 + (1 - core), "grp": z}

    def on_chip(c):
        return {"rows": c * 2 + core, "grp": z}

    def on_plane(k):
        return {"rows": r, "grp": k}

    def remote(src, dst, send, recv, device):
        return pltpu.make_async_remote_copy(
            src_ref=src, dst_ref=dst, send_sem=send, recv_sem=recv, device_id=device, device_id_type=MESH
        )

    barrier = pltpu.get_barrier_semaphore()
    partners = [partner] + [on_chip(c) for c in plane_chips] + [on_plane(k) for k in other_planes]
    for device in partners:
        pl.semaphore_signal(barrier, inc=1, device_id=device, device_id_type=MESH)

    load_b = pltpu.make_async_copy(b_hbm, b, load_sem.at[0])
    load_a = pltpu.make_async_copy(a_hbm, a, load_sem.at[1])
    load_n = pltpu.make_async_copy(n_hbm, n, load_sem.at[2])
    load_b.start()
    load_a.start()
    load_n.start()

    live = (lax.broadcasted_iota(jnp.int32, (columns, rows), 1) < count_ref[0]).astype(jnp.float32)
    ones = jnp.ones((8, rows), jnp.bfloat16)

    def keep_squares(residue):
        square = residue * residue
        high = square.astype(jnp.bfloat16)
        low = (square - high.astype(jnp.float32)).astype(jnp.bfloat16)
        total = dot_nt(ones, high) + dot_nt(ones, low)
        csq[0] = total[0:1]

    def keep_residue(residue):
        pref[...] = residue
        pb[...] = residue.astype(jnp.bfloat16)
        keep_squares(residue)

    rv[...] = jnp.zeros_like(rv)
    search[...] = jnp.zeros_like(search)
    coeffs[...] = jnp.zeros_like(coeffs)
    rho[...] = jnp.zeros_like(rho)
    phi[...] = jnp.zeros_like(phi)
    start[...] = jnp.zeros_like(start)

    load_b.wait()
    keep_residue(live * jnp.transpose(b[...].astype(jnp.float32)))
    load_a.wait()
    pl.semaphore_wait(barrier, len(partners))

    def core_copy(j):
        theirs = pl.ds((1 - core) * half, half)
        block = pl.ds(j * per_tile, per_tile)
        return remote(partb.at[block, theirs], crecv.at[block], cs_sem.at[j], cr_sem.at[j], partner)

    core_sq = remote(csq.at[0], csq.at[1], csqs_sem, csqr_sem, partner)

    def plane_copy(c):
        return remote(xsend.at[c], xrecv.at[chip], xs_sem.at[c], xr_sem.at[chip], on_chip(c))

    def plane_arrival(c):
        return remote(xsend.at[c], xrecv.at[c], xs_sem.at[c], xr_sem.at[c], on_chip(c))

    def plane_sq(c):
        return remote(xsq.at[chip], xsq.at[chip], xsqs_sem.at[c], xsqr_sem.at[chip], on_chip(c))

    def plane_sq_arrival(c):
        return remote(xsq.at[c], xsq.at[c], xsqs_sem.at[c], xsqr_sem.at[c], on_chip(c))

    def depth_copy(par, k):
        return remote(zbuf.at[par, z], zbuf.at[par, z], zs_sem.at[par, k], zr_sem.at[par, z], on_plane(k))

    def depth_arrival(par, k):
        return remote(zbuf.at[par, k], zbuf.at[par, k], zs_sem.at[par, k], zr_sem.at[par, k], on_plane(k))

    def depth_sq(par, k):
        return remote(zsq.at[par, z], zsq.at[par, z], zsqs_sem.at[par, k], zsqr_sem.at[par, z], on_plane(k))

    def depth_sq_arrival(par, k):
        return remote(zsq.at[par, k], zsq.at[par, k], zsqs_sem.at[par, k], zsqr_sem.at[par, k], on_plane(k))

    def piece(c, h):
        return q.at[pl.ds(pl.multiple_of(h * half, half), half), pl.ds(pl.multiple_of(c * LANES, LANES), LANES)]

    def gather_copy(c):
        return remote(piece(chip, core), piece(chip, core), gs_sem.at[c], gr_sem.at[chip], on_chip(c))

    def gather_arrival(c):
        return remote(piece(c, core), piece(c, core), gs_sem.at[c], gr_sem.at[c], on_chip(c))

    def forward_copy(c):
        return remote(piece(c, core), piece(c, core), fs_sem.at[c], fr_sem.at[c], partner)

    def forward_arrival(c):
        return remote(piece(c, 1 - core), piece(c, 1 - core), fs_sem.at[c], fr_sem.at[c], partner)

    def squares_plane():
        core_sq.wait_recv()
        xsq[chip] = csq[0] + csq[1]
        for c in plane_chips:
            plane_sq(c).start()

    def squares_depth(par):
        for c in plane_chips:
            plane_sq_arrival(c).wait_recv()
        total = xsq[0]
        for c in range(1, CHIPS):
            total = total + xsq[c]
        zsq[par, z] = total
        for k in other_planes:
            depth_sq(par, k).start()

    def squares_total(par):
        for k in other_planes:
            depth_sq_arrival(par, k).wait_recv()
        total = zsq[par, 0]
        for k in range(1, planes):
            total = total + zsq[par, k]
        spread = jnp.transpose(jnp.broadcast_to(total, (columns, columns)))
        ucol[...] = jnp.sqrt(spread + FLOOR_SQ)

    def squares_sent(par):
        core_sq.wait_send()
        for c in plane_chips:
            plane_sq(c).wait_send()
        for k in other_planes:
            depth_sq(par, k).wait_send()

    mine = pl.ds(pl.multiple_of(z * own_cols, own_cols), own_cols)

    def turn(i, carry):
        par = lax.rem(i, 2)

        core_sq.start()
        residue = pb[...]
        for j in range(tiles):
            product = dot(residue, a[:, j * TILE : (j + 1) * TILE])
            for s in range(per_tile):
                chunk = product[:, s * LANES : (s + 1) * LANES]
                part[j * per_tile + s] = chunk
                partb[j * per_tile + s] = chunk.astype(jnp.bfloat16)
            if j:
                core_copy(j - 1).start()
        core_copy(tiles - 1).start()

        @pl.when(i == 0)
        def _():
            load_n.wait()

        ours = pl.ds(pl.multiple_of(core * half, half), half)
        for j in range(tiles):
            core_copy(j).wait_recv()
        before = None
        for c in plane_chips:
            xsend[c] = (part[c, ours] + crecv[c].astype(jnp.float32)).astype(jnp.bfloat16)
            if before is not None:
                plane_copy(before).start()
            before = c
        own = part[chip, ours] + crecv[chip].astype(jnp.float32)
        plane_copy(before).start()
        squares_plane()
        for c in reversed(plane_chips):
            plane_arrival(c).wait_recv()
            own = own + xrecv[c].astype(jnp.float32)
        zbuf[par, z] = own.astype(jnp.bfloat16)
        squares_depth(par)
        for k in other_planes:
            depth_copy(par, k).start()

        squares_total(par)
        for k in reversed(other_planes):
            depth_arrival(par, k).wait_recv()
        total = zbuf[par, 0].astype(jnp.float32)
        for k in range(1, planes):
            total = total + zbuf[par, k].astype(jnp.float32)
        scaled = (total / ucol[ours]).astype(jnp.bfloat16)
        q[ours, pl.ds(pl.multiple_of(chip * LANES, LANES), LANES)] = scaled

        for c in plane_chips:
            gather_copy(c).start()
        forward_copy(chip).start()
        for c in reversed(plane_chips):
            gather_arrival(c).wait_recv()
            forward_copy(c).start()
        for j in range(tiles):
            core_copy(j).wait_send()
        for c in plane_chips:
            plane_copy(c).wait_send()
        for k in other_planes:
            depth_copy(par, k).wait_send()
        squares_sent(par)
        forward_arrival(chip).wait_recv()
        for c in reversed(plane_chips):
            forward_arrival(c).wait_recv()

        u = ucol[...]
        u_tile = wide(u, per_tile)
        gathered = q[...]
        squares = jnp.zeros((columns, LANES), jnp.float32)
        for j in range(tiles):
            at = slice(j * TILE, (j + 1) * TILE)
            raw = dot(gathered, n[:, at]) - u_tile * rv[:, at]
            rv[:, at] = raw
            for s in range(per_tile):
                block = raw[:, s * LANES : (s + 1) * LANES]
                squares = squares + block * block
        v = jnp.sqrt(jnp.sum(squares, axis=1, keepdims=True) + FLOOR_SQ)
        v = jnp.broadcast_to(v, (columns, LANES))
        vcol[...] = v
        v_tile = wide(v, per_tile)
        for j in range(tiles):
            at = slice(j * TILE, (j + 1) * TILE)
            unit = rv[:, at] / v_tile
            rv[:, at] = unit
            vb[:, at] = unit.astype(jnp.bfloat16)

        unit = vb[...]
        for j in range(tiles):
            at = slice(j * TILE, (j + 1) * TILE)
            pushed[:, at] = dot_nt(unit, n[at, :]).astype(jnp.bfloat16)
        front = pushed[...]
        image = jnp.concatenate(
            [dot_nt(front, a[j * TILE : (j + 1) * TILE, :]) for j in range(rows // TILE)], axis=1
        )
        keep_residue(live * (image - wide(v / u, rows // LANES) * pref[...]))

        u_own = ucol[mine]
        first = i == 0
        unit_own = rv[mine]
        v_own = vcol[mine]
        radius = jnp.sqrt(rho[...] * rho[...] + u_own * u_own)
        cosine = rho[...] / radius
        sine = u_own / radius
        coupling = sine * v_own
        phi_step = cosine * phi[...]
        coeffs[...] = coeffs[...] + wide(phi_step / radius, width // LANES) * search[...]
        search[...] = unit_own - wide(coupling / radius, width // LANES) * search[...]
        rho[...] = jnp.where(first, v_own, -cosine * v_own)
        phi[...] = jnp.where(first, u_own, sine * phi[...])
        start[...] = jnp.where(first, u_own, start[...])

        for c in plane_chips:
            gather_copy(c).wait_send()
            forward_copy(c).wait_send()
        forward_copy(chip).wait_send()
        return carry

    lax.fori_loop(0, ITERS, turn, 0)

    par = ITERS % 2
    core_sq.start()
    squares_plane()
    squares_depth(par)
    squares_total(par)
    squares_sent(par)
    u_own = ucol[mine]
    radius = jnp.sqrt(rho[...] * rho[...] + u_own * u_own)
    cosine = rho[...] / radius
    sine = u_own / radius
    result = coeffs[...] + wide(cosine * phi[...] / radius, width // LANES) * search[...]
    coef_ref[...] = result
    ratio_ref[...] = sine * phi[...] / start[...]
    narrow = result.astype(jnp.bfloat16)
    for j in range(tiles):
        at = slice(j * TILE, (j + 1) * TILE)
        sol_ref[:, at] = dot_nt(narrow, n[at, :])


def shards(planes, matrix, right_side, precond, row_counts):
    rows, width = matrix.shape
    columns = right_side.shape[1]
    own_cols = columns // planes
    half = columns // 2
    tiles = width // TILE
    vmem, dma = pltpu.VMEM, pltpu.SemaphoreType.DMA
    bf16, f32 = jnp.bfloat16, jnp.float32
    solution, coeffs, ratio = pl.pallas_call(
        functools.partial(kernel, planes),
        out_shape=(
            jax.ShapeDtypeStruct((own_cols, width), f32),
            jax.ShapeDtypeStruct((own_cols, width), f32),
            jax.ShapeDtypeStruct((own_cols, LANES), f32),
        ),
        in_specs=[pl.BlockSpec(memory_space=pltpu.SMEM)] + [pl.BlockSpec(memory_space=pl.ANY)] * 3,
        out_specs=(pl.BlockSpec(memory_space=vmem),) * 3,
        scratch_shapes=[
            vmem((rows, width), bf16),
            vmem((rows, columns), bf16),
            vmem((width, width), bf16),
            vmem((columns, width), f32),
            vmem((columns, width), bf16),
            vmem((columns, width), bf16),
            vmem((columns, rows), f32),
            vmem((columns, rows), bf16),
            vmem((columns, width), bf16),
            vmem((CHIPS, columns, LANES), f32),
            vmem((CHIPS, columns, LANES), bf16),
            vmem((CHIPS, half, LANES), bf16),
            vmem((CHIPS, half, LANES), bf16),
            vmem((CHIPS, half, LANES), bf16),
            vmem((2, planes, half, LANES), bf16),
            vmem((2, 1, columns), f32),
            vmem((CHIPS, 1, columns), f32),
            vmem((2, planes, 1, columns), f32),
            vmem((own_cols, width), f32),
            vmem((own_cols, width), f32),
            vmem((own_cols, LANES), f32),
            vmem((own_cols, LANES), f32),
            vmem((own_cols, LANES), f32),
            vmem((columns, LANES), f32),
            vmem((columns, LANES), f32),
            dma((3,)),
            dma((tiles,)), dma((tiles,)),
            dma((CHIPS,)), dma((CHIPS,)),
            dma((2, planes)), dma((2, planes)),
            dma((CHIPS,)), dma((CHIPS,)),
            dma((CHIPS,)), dma((CHIPS,)),
            dma, dma,
            dma((CHIPS,)), dma((CHIPS,)),
            dma((2, planes)), dma((2, planes)),
        ],
        compiler_params=pltpu.CompilerParams(
            collective_id=0, has_side_effects=True, vmem_limit_bytes=60 * 1024 * 1024
        ),
    )(row_counts, matrix, right_side, precond)
    return solution.T, coeffs.T, ratio[:, 0]


def solution(mesh):
    return jax.shard_map(
        functools.partial(shards, mesh.shape["grp"]),
        mesh=mesh,
        in_specs=(P(("rows", "grp"), None), P(("rows", "grp"), None), P(), P(("rows", "grp"))),
        out_specs=(P(None, "grp"), P(None, "grp"), P("grp")),
        check_vma=False,
    )
```

time: 402 us -> 106 us (0.26)
  blocking collectives: 233 us -> 0 us
  Pallas kernels: 0 us -> 99.4 us
  waiting for transfers between devices: 55.7 us -> 0 us
  matrix products: 42.8 us -> 0 us
  starting transfers between devices: 27.3 us -> 0 us
  local copies, waits for them, and re-layouts: 30.4 us -> 4.46 us
  other arithmetic: 9.51 us -> 0 us
    all_to_all x12 -> x0, blocking collectives: 233 us -> none  [the longest x8 188 us: sent_and_summed(): tiles = lax.all_to_all(cut_along(value, dim, peers), axis, 0, 0, tiled=True)]
    pallas_call x0 -> x1, Pallas kernels: none -> 99.4 us  [shards(): pl.pallas_call(functools.partial(kernel, planes), out_shape=(jax.ShapeDty...]
    all_to_all x6 -> x0, waiting for transfers between devices: 55.7 us -> none  [copy_for_each(): return lax.all_to_all(copies, axis, split_axis=0, concat_axis=0, tiled=True)]
    dot_general x14 -> x0, matrix products: 42.8 us -> none  [the longest x3 17.1 us: share_cols(): jnp.dot(precond, right_vec.astype(jnp.bfloat16), preferred_element_type=j...]
    all_to_all x6 -> x0, starting transfers between devices: 27.3 us -> none  [copy_for_each(): return lax.all_to_all(copies, axis, split_axis=0, concat_axis=0, tiled=True)]
    slice x18 -> x1, local copies, waits for them, and re-layouts: 14.3 us -> 1.32 us  [shards(): return (solution.T, coeffs.T, ratio[:, 0])]
    reshape x8 -> x0, local copies, waits for them, and re-layouts: 5.94 us -> none  [the longest x4 3.4 us: joined_along(): return jnp.moveaxis(tiles, 0, dim).reshape(lengths)]
    broadcast_in_dim x10 -> x0, local copies, waits for them, and re-layouts: 4.65 us -> none  [copy_for_each(): copies = jnp.broadcast_to(value, (lax.axis_size(axis), *value.shape))]
  transfers between devices with their start and end apart: 6 -> 0, of which waited for: 6 -> 0; matrix products, arithmetic and copies ran while one was open for 4% -> 0% of each run, Pallas kernels for 0% -> 0%
where the time goes in v1:
time: 106 us; the launch traced here: 105 us
  Pallas kernels  99.4 us (94%)
  local copies, waits for them, and re-layouts  4.46 us (4%)
  between operations  1.29 us (1%)
    pallas_call x1, Pallas kernels, shards(): pl.pallas_call(functools.partial(kernel, planes), out_shape=(jax.ShapeDty...  99.4 us
    unnamed x2, local copies, waits for them, and re-layouts  3.13 us

profile of v1, /device:TPU:1, one launch (start us, length us, event | category | flops | bytes accessed | tf_op | source)
XLA Modules:
  0.0 105.1 jit_solution(16264221075377405144)
XLA Ops:
  1.3 99.4 %shard_map.67 = (f32[16,2048]{1,0:T(8,128)}, f32[16,2048]{1,0:T(8,128)}, f32[16,128]{1,0:T(8,128)}) custom-call(s32[1]{0:T(128)S(6)} %copy.9.count_ref, bf16[512,2048]{1,0:T(8,128)(2,1)} %a_hbm.1, bf16[512,128]{1,0:T(8,128)(2,1)} %b_hbm.1, bf16[2048,2048]{1,0:T(8,128)(2,1)} %n_hbm.1), custom_call_target="tpu_custom_call" | custom-call | tf_op jit(solution)/shard_map/pallas_call | solution.py:349
  100.7 1.3 %slice_reduce_fusion = f32[16]{0:T(128)} fusion(f32[16,128]{1,0:T(8,128)} %get-tuple-element.8), kind=kLoop, calls=%fused_computation | loop fusion | bytes 128 | tf_op jit(solution)/shard_map/slice | solution.py:398
  102.0 1.6 %copy.10 = f32[2048,16]{0,1:T(8,128)} copy(f32[2048,16]{0,1:T(8,128)} %bitcast.3) | data formatting | bytes 262144
  103.6 1.6 %copy.11 = f32[2048,16]{0,1:T(8,128)} copy(f32[2048,16]{0,1:T(8,128)} %bitcast.2) | data formatting | bytes 262144

commit v2 on v1

v2 whole, which is shorter than its diff:
```python
import functools

import jax
import jax.numpy as jnp
from jax import lax
from jax.experimental import pallas as pl
from jax.experimental.pallas import tpu as pltpu
from jax.sharding import PartitionSpec as P

ITERS = 3
FLOOR_SQ = 0.01
MESH = pl.DeviceIdType.MESH
SIDE = 4
CHIPS = SIDE * SIDE
LANES = 128
TILE = 256
GROUP = SIDE * LANES

SEND_ROWS = (2, 1, 3, 0)
SEND_COLS = (2, 1, 3, 0)
TAKE_ROWS = (2, 1, 3, 0)

NT = (((1,), (1,)), ((), ()))


def dot(a, b):
    return jnp.dot(a, b, preferred_element_type=jnp.float32)


def dot_nt(a, b):
    return lax.dot_general(a, b, NT, preferred_element_type=jnp.float32)


def wide(column, count):
    return jnp.concatenate([column] * count, axis=1)


def halves(value):
    high = value.astype(jnp.bfloat16)
    return high, (value - high.astype(jnp.float32)).astype(jnp.bfloat16)


def kernel(
    planes,
    count_ref, a_hbm, b_hbm, n_hbm,
    sol_ref, coef_ref, ratio_ref,
    a, at, b, n, nt, rv, raw, vb, pushed, pref, pb, p0, q, part, partb, crecv, xsend, xrecv, ownrow, zbuf,
    live, csq, xsq, zsq, fsq, state, scalars, ucol, vcol,
    load_sem, cs_sem, cr_sem, ps_sem, pr_sem, ls_sem, lr_sem, as_sem, ar_sem,
    xs_sem, xr_sem, zs_sem, zr_sem, gs_sem, gr_sem,
    xsqs_sem, xsqr_sem, zsqs_sem, zsqr_sem, fsqs_sem, fsqr_sem, ts_sem, tr_sem, us_sem, ur_sem,
):
    half, width = rv.shape
    columns = 2 * half
    rows = b.shape[0]
    both = 2 * rows
    own_cols = columns // planes
    per_core = planes // 2

    r = lax.axis_index("rows")
    z = lax.axis_index("grp")
    core = lax.rem(r, 2)
    chip = lax.div(r, 2)
    x = lax.rem(chip, SIDE)
    y = lax.div(chip, SIDE)

    def row_at(dy):
        return lax.rem(y + dy, SIDE)

    def chip_at(dy, dx):
        return row_at(dy) * SIDE + lax.rem(x + dx, SIDE)

    offsets = [(dy, dx) for dy in SEND_ROWS for dx in SEND_COLS if dy or dx]
    plane_chips = [chip_at(dy, dx) for dy, dx in offsets]
    other_planes = [lax.rem(z + k, planes) for k in sorted(range(1, planes), key=lambda k: -min(k, planes - k))]
    partner = {"rows": chip * 2 + (1 - core), "grp": z}

    def on_chip(c):
        return {"rows": c * 2 + core, "grp": z}

    def on_plane(k, other=False):
        return {"rows": chip * 2 + (1 - core) if other else r, "grp": k}

    def remote(src, dst, send, recv, device):
        return pltpu.make_async_remote_copy(
            src_ref=src, dst_ref=dst, send_sem=send, recv_sem=recv, device_id=device, device_id_type=MESH
        )

    barrier = pltpu.get_barrier_semaphore()
    partners = (
        [partner]
        + [on_chip(c) for c in plane_chips]
        + [on_plane(k) for k in other_planes]
        + [on_plane(k, True) for k in other_planes]
    )
    for device in partners:
        pl.semaphore_signal(barrier, inc=1, device_id=device, device_id_type=MESH)

    load_b = pltpu.make_async_copy(b_hbm, b, load_sem.at[0])
    load_a = pltpu.make_async_copy(a_hbm, a.at[pl.ds(0, rows)], load_sem.at[1])
    load_n = pltpu.make_async_copy(n_hbm, n, load_sem.at[2])
    load_b.start()
    load_a.start()
    load_n.start()

    ours = pl.ds(pl.multiple_of(core * half, half), half)
    theirs = pl.ds(pl.multiple_of((1 - core) * half, half), half)
    ones = jnp.ones((8, both), jnp.bfloat16)

    core_copy = remote(partb.at[theirs], crecv, cs_sem, cr_sem, partner)
    residue_copy = remote(p0.at[theirs], p0.at[pl.ds(columns, half)], ps_sem, pr_sem, partner)
    live_copy = remote(live.at[0], live.at[1], ls_sem, lr_sem, partner)
    a_copy = remote(a.at[pl.ds(0, rows)], a.at[pl.ds(rows, rows)], as_sem, ar_sem, partner)
    state_copy = remote(state.at[core], state.at[core], ts_sem, tr_sem, partner)
    state_arrival = remote(state.at[1 - core], state.at[1 - core], ts_sem, tr_sem, partner)
    scalars_copy = remote(scalars.at[core], scalars.at[core], us_sem, ur_sem, partner)
    scalars_arrival = remote(scalars.at[1 - core], scalars.at[1 - core], us_sem, ur_sem, partner)

    def plane_copy(c):
        return remote(xsend.at[c], xrecv.at[chip], xs_sem.at[c], xr_sem.at[chip], on_chip(c))

    def plane_arrival(c):
        return remote(xsend.at[c], xrecv.at[c], xs_sem.at[c], xr_sem.at[c], on_chip(c))

    def plane_sq(c):
        return remote(xsq.at[chip], xsq.at[chip], xsqs_sem.at[c], xsqr_sem.at[chip], on_chip(c))

    def plane_sq_arrival(c):
        return remote(xsq.at[c], xsq.at[c], xsqs_sem.at[c], xsqr_sem.at[c], on_chip(c))

    def depth_copy(par, k):
        return remote(zbuf.at[par, z], zbuf.at[par, z], zs_sem.at[par, k], zr_sem.at[par, z], on_plane(k))

    def depth_arrival(par, k):
        return remote(zbuf.at[par, k], zbuf.at[par, k], zs_sem.at[par, k], zr_sem.at[par, k], on_plane(k))

    def depth_sq(par, k):
        return remote(zsq.at[par, z], zsq.at[par, z], zsqs_sem.at[par, k], zsqr_sem.at[par, z], on_plane(k))

    def depth_sq_arrival(par, k):
        return remote(zsq.at[par, k], zsq.at[par, k], zsqs_sem.at[par, k], zsqr_sem.at[par, k], on_plane(k))

    def last_sq(k, other):
        there = (1 - core) if other else core
        return remote(fsq.at[core, z], fsq.at[core, z], fsqs_sem.at[there, k], fsqr_sem.at[core, z], on_plane(k, other))

    def last_sq_arrival(h, k):
        return remote(fsq.at[h, k], fsq.at[h, k], fsqs_sem.at[h, k], fsqr_sem.at[h, k], partner)

    def piece(c):
        return q.at[:, pl.ds(pl.multiple_of(c * LANES, LANES), LANES)]

    def gather_copy(c):
        return remote(piece(chip), piece(chip), gs_sem.at[c], gr_sem.at[chip], on_chip(c))

    def gather_arrival(c):
        return remote(piece(c), piece(c), gs_sem.at[c], gr_sem.at[c], on_chip(c))

    def keep_squares():
        square = pref[...] * pref[...]
        blank = jnp.zeros_like(square)
        square = jnp.concatenate(
            [jnp.where(core == 0, square, blank), jnp.where(core == 0, blank, square)], axis=0
        )
        high, low = halves(square)
        total = dot_nt(ones, high) + dot_nt(ones, low)
        csq[...] = total[0:1]

    def squares_plane():
        xsq[chip] = csq[...]
        for c in plane_chips:
            plane_sq(c).start()

    def squares_of_plane():
        for c in plane_chips:
            plane_sq_arrival(c).wait_recv()
        total = xsq[0]
        for c in range(1, CHIPS):
            total = total + xsq[c]
        return total

    def keep_norm(total):
        spread = jnp.transpose(jnp.broadcast_to(total, (columns, columns)))
        ucol[...] = jnp.sqrt(spread + FLOOR_SQ)

    def send_group(value, dy):
        line = row_at(dy) * SIDE
        for s in range(SIDE):
            block = value[:, s * LANES : (s + 1) * LANES]
            xsend[line + s] = block.astype(jnp.bfloat16)
            if dy == 0:
                ownrow[s] = block
        for dx in SEND_COLS:
            if dy or dx:
                plane_copy(chip_at(dy, dx)).start()

    rv[...] = jnp.zeros_like(rv)
    state[...] = jnp.zeros_like(state)
    scalars[...] = jnp.zeros_like(scalars)
    shown = (lax.broadcasted_iota(jnp.int32, (1, rows), 1) < count_ref[0]).astype(jnp.float32)
    live[0] = shown
    load_b.wait()
    first_residue = shown * jnp.transpose(b[...].astype(jnp.float32))
    p0[pl.ds(0, columns)] = first_residue.astype(jnp.bfloat16)
    load_a.wait()

    start_residue = p0[pl.ds(0, columns)]
    for j in range(width // TILE):
        lanes = slice(j * TILE, (j + 1) * TILE)
        product = dot(start_residue, a[pl.ds(0, rows), lanes])
        part[:, lanes] = product
        partb[:, lanes] = product.astype(jnp.bfloat16)
    pl.semaphore_wait(barrier, len(partners))
    core_copy.start()
    residue_copy.start()
    live_copy.start()
    a_copy.start()

    mine = pl.ds(pl.multiple_of(lax.rem(z, per_core) * own_cols, own_cols), own_cols)
    spread = width // LANES

    def turn(i, carry):
        par = lax.rem(i, 2)

        @pl.when(i == 0)
        def _():
            core_copy.wait_recv()
            for dy in SEND_ROWS:
                lanes = pl.ds(pl.multiple_of(row_at(dy) * GROUP, GROUP), GROUP)
                send_group(part[ours, lanes] + crecv[:, lanes].astype(jnp.float32), dy)
            residue_copy.wait_recv()
            pref[...] = jnp.concatenate([p0[ours], p0[pl.ds(columns, half)]], axis=1).astype(jnp.float32)
            keep_squares()

        @pl.when(i > 0)
        def _():
            residue = pb[...]
            for dy in SEND_ROWS:
                lanes = pl.ds(pl.multiple_of(row_at(dy) * GROUP, GROUP), GROUP)
                send_group(dot(residue, a[:, lanes]), dy)

        squares_plane()

        @pl.when(i == 0)
        def _():
            lines = lax.broadcasted_iota(jnp.int32, (TILE, TILE), 0)
            same = (lines == lax.broadcasted_iota(jnp.int32, (TILE, TILE), 1)).astype(jnp.bfloat16)
            load_n.wait()

            def flip_n(k, c):
                here = pl.ds(pl.multiple_of(k * TILE, TILE), TILE)
                for j in range(width // TILE):
                    lanes = slice(j * TILE, (j + 1) * TILE)
                    nt[lanes, here] = dot_nt(same, n[here, lanes]).astype(jnp.bfloat16)
                return c

            lax.fori_loop(0, width // TILE, flip_n, 0)

        own = ownrow[x]
        for c in plane_chips:
            plane_arrival(c).wait_recv()
            own = own + xrecv[c].astype(jnp.float32)
        zbuf[par, z] = own.astype(jnp.bfloat16)
        zsq[par, z] = squares_of_plane()
        for k in other_planes:
            depth_copy(par, k).start()
            depth_sq(par, k).start()

        @pl.when(i == 0)
        def _():
            lines = lax.broadcasted_iota(jnp.int32, (TILE, TILE), 0)
            same = (lines == lax.broadcasted_iota(jnp.int32, (TILE, TILE), 1)).astype(jnp.bfloat16)
            a_copy.wait_recv()
            live_copy.wait_recv()

            def flip_a(k, c):
                here = pl.ds(pl.multiple_of(k * TILE, TILE), TILE)
                for j in range(width // TILE):
                    lanes = slice(j * TILE, (j + 1) * TILE)
                    at[lanes, here] = dot_nt(same, a[here, lanes]).astype(jnp.bfloat16)
                return c

            lax.fori_loop(0, both // TILE, flip_a, 0)

        for k in other_planes:
            depth_sq_arrival(par, k).wait_recv()
        total = zsq[par, 0]
        for k in range(1, planes):
            total = total + zsq[par, k]
        keep_norm(total)
        u = ucol[ours]
        for k in other_planes:
            depth_arrival(par, k).wait_recv()
        total = zbuf[par, 0].astype(jnp.float32)
        for k in range(1, planes):
            total = total + zbuf[par, k].astype(jnp.float32)
        q[:, pl.ds(pl.multiple_of(chip * LANES, LANES), LANES)] = (total / u).astype(jnp.bfloat16)

        for c in plane_chips:
            gather_copy(c).start()
        u_tile = wide(u, TILE // LANES)
        squares = jnp.zeros((half, LANES), jnp.float32)
        for turn_at, dy in enumerate(TAKE_ROWS):
            for dx in SEND_COLS:
                if dy or dx:
                    gather_arrival(chip_at(dy, dx)).wait_recv()
            here = pl.ds(pl.multiple_of(row_at(dy) * GROUP, GROUP), GROUP)
            taken = q[:, here]
            for j in range(width // TILE):
                lanes = slice(j * TILE, (j + 1) * TILE)
                before = raw[:, lanes] if turn_at else -u_tile * rv[:, lanes]
                value = before + dot(taken, n[here, lanes])
                raw[:, lanes] = value
                if turn_at == SIDE - 1:
                    for s in range(TILE // LANES):
                        block = value[:, s * LANES : (s + 1) * LANES]
                        squares = squares + block * block
        v = jnp.sqrt(jnp.sum(squares, axis=1, keepdims=True) + FLOOR_SQ)
        v = jnp.broadcast_to(v, (half, LANES))
        vcol[...] = v
        inverse = wide(1.0 / v, TILE // LANES)
        for j in range(width // TILE):
            lanes = slice(j * TILE, (j + 1) * TILE)
            unit = raw[:, lanes] * inverse
            rv[:, lanes] = unit
            vb[:, lanes] = unit.astype(jnp.bfloat16)

        unit = vb[...]
        for j in range(width // TILE):
            lanes = slice(j * TILE, (j + 1) * TILE)
            pushed[:, lanes] = dot(unit, nt[:, lanes]).astype(jnp.bfloat16)
        front = pushed[...]
        back = wide(v / u, rows // LANES)
        for h in range(2):
            lanes = slice(h * rows, (h + 1) * rows)
            residue = live[h] * (dot(front, at[:, lanes]) - back * pref[:, lanes])
            pref[:, lanes] = residue
            pb[:, lanes] = residue.astype(jnp.bfloat16)

        for c in plane_chips:
            plane_copy(c).wait_send()
            plane_sq(c).wait_send()
        keep_squares()

        first = i == 0
        u_own = ucol[pl.ds(pl.multiple_of(core * half, half) + lax.rem(z, per_core) * own_cols, own_cols)]
        v_own = vcol[mine]
        rho, phi, start = (scalars[core, pl.ds(k * own_cols, own_cols)] for k in range(3))
        search = state[core, pl.ds(own_cols, own_cols)]
        radius = jnp.sqrt(rho * rho + u_own * u_own)
        cosine = rho / radius
        sine = u_own / radius
        state[core, pl.ds(0, own_cols)] = (
            state[core, pl.ds(0, own_cols)] + wide(cosine * phi / radius, spread) * search
        )
        state[core, pl.ds(own_cols, own_cols)] = rv[mine] - wide(sine * v_own / radius, spread) * search
        scalars[core, pl.ds(0, own_cols)] = jnp.where(first, v_own, -cosine * v_own)
        scalars[core, pl.ds(own_cols, own_cols)] = jnp.where(first, u_own, sine * phi)
        scalars[core, pl.ds(2 * own_cols, own_cols)] = jnp.where(first, u_own, start)

        for k in other_planes:
            depth_copy(par, k).wait_send()
            depth_sq(par, k).wait_send()
        for c in plane_chips:
            gather_copy(c).wait_send()
        return carry

    lax.fori_loop(0, ITERS, turn, 0)

    squares_plane()
    state_copy.start()
    scalars_copy.start()
    fsq[core, z] = squares_of_plane()
    last_core = remote(fsq.at[core, z], fsq.at[core, z], fsqs_sem.at[1 - core, z], fsqr_sem.at[core, z], partner)
    for k in other_planes:
        last_sq(k, False).start()
        last_sq(k, True).start()
    last_core.start()

    holder = lax.div(z, per_core)
    state_arrival.wait_recv()
    scalars_arrival.wait_recv()
    high, low = halves(state[holder])
    stacked = jnp.concatenate([high, low], axis=0)
    for j in range(width // TILE):
        lanes = slice(j * TILE, (j + 1) * TILE)
        product = dot(stacked, nt[:, lanes])
        raw[pl.ds(0, 2 * own_cols), lanes] = product[: 2 * own_cols] + product[2 * own_cols :]

    last_sq_arrival(1 - core, z).wait_recv()
    for k in other_planes:
        last_sq_arrival(0, k).wait_recv()
        last_sq_arrival(1, k).wait_recv()
    total = fsq[0, 0]
    for h in range(2):
        for k in range(planes):
            if h or k:
                total = total + fsq[h, k]
    keep_norm(total)
    u_own = ucol[pl.ds(pl.multiple_of(z * own_cols, own_cols), own_cols)]
    rho, phi, start = (scalars[holder, pl.ds(k * own_cols, own_cols)] for k in range(3))
    radius = jnp.sqrt(rho * rho + u_own * u_own)
    cosine = rho / radius
    sine = u_own / radius
    step = wide(cosine * phi / radius, spread)
    coef_ref[...] = state[holder, pl.ds(0, own_cols)] + step * state[holder, pl.ds(own_cols, own_cols)]
    sol_ref[...] = raw[pl.ds(0, own_cols)] + step * raw[pl.ds(own_cols, own_cols)]
    ratio_ref[...] = sine * phi / start

    for copy in (core_copy, residue_copy, live_copy, a_copy, state_copy, scalars_copy, last_core):
        copy.wait_send()
    for c in plane_chips:
        plane_sq(c).wait_send()
    for k in other_planes:
        last_sq(k, False).wait_send()
        last_sq(k, True).wait_send()


def shards(planes, matrix, right_side, precond, row_counts):
    rows, width = matrix.shape
    columns = right_side.shape[1]
    own_cols = columns // planes
    half = columns // 2
    vmem, dma = pltpu.VMEM, pltpu.SemaphoreType.DMA
    bf16, f32 = jnp.bfloat16, jnp.float32
    solution, coeffs, ratio = pl.pallas_call(
        functools.partial(kernel, planes),
        out_shape=(
            jax.ShapeDtypeStruct((own_cols, width), f32),
            jax.ShapeDtypeStruct((own_cols, width), f32),
            jax.ShapeDtypeStruct((own_cols, LANES), f32),
        ),
        in_specs=[pl.BlockSpec(memory_space=pltpu.SMEM)] + [pl.BlockSpec(memory_space=pl.ANY)] * 3,
        out_specs=(pl.BlockSpec(memory_space=vmem),) * 3,
        scratch_shapes=[
            vmem((2 * rows, width), bf16),
            vmem((width, 2 * rows), bf16),
            vmem((rows, columns), bf16),
            vmem((width, width), bf16),
            vmem((width, width), bf16),
            vmem((half, width), f32),
            vmem((half, width), f32),
            vmem((half, width), bf16),
            vmem((half, width), bf16),
            vmem((half, 2 * rows), f32),
            vmem((half, 2 * rows), bf16),
            vmem((columns + half, rows), bf16),
            vmem((half, width), bf16),
            vmem((columns, width), f32),
            vmem((columns, width), bf16),
            vmem((half, width), bf16),
            vmem((CHIPS, half, LANES), bf16),
            vmem((CHIPS, half, LANES), bf16),
            vmem((SIDE, half, LANES), f32),
            vmem((2, planes, half, LANES), bf16),
            vmem((2, 1, rows), f32),
            vmem((1, columns), f32),
            vmem((CHIPS, 1, columns), f32),
            vmem((2, planes, 1, columns), f32),
            vmem((2, planes, 1, columns), f32),
            vmem((2, 2 * own_cols, width), f32),
            vmem((2, 3 * own_cols, LANES), f32),
            vmem((columns, LANES), f32),
            vmem((half, LANES), f32),
            dma((3,)),
            dma, dma, dma, dma, dma, dma, dma, dma,
            dma((CHIPS,)), dma((CHIPS,)),
            dma((2, planes)), dma((2, planes)),
            dma((CHIPS,)), dma((CHIPS,)),
            dma((CHIPS,)), dma((CHIPS,)),
            dma((2, planes)), dma((2, planes)),
            dma((2, planes)), dma((2, planes)),
            dma, dma, dma, dma,
        ],
        compiler_params=pltpu.CompilerParams(
            collective_id=0, has_side_effects=True, vmem_limit_bytes=60 * 1024 * 1024
        ),
    )(row_counts, matrix, right_side, precond)
    return solution.T, coeffs.T, ratio[:, 0]


def solution(mesh):
    return jax.shard_map(
        functools.partial(shards, mesh.shape["grp"]),
        mesh=mesh,
        in_specs=(P(("rows", "grp"), None), P(("rows", "grp"), None), P(), P(("rows", "grp"))),
        out_specs=(P(None, "grp"), P(None, "grp"), P("grp")),
        check_vma=False,
    )
```

time: 106 us -> 92.8 us (0.88)
  Pallas kernels: 99.4 us -> 86.9 us
    pallas_call x1, Pallas kernels: 99.4 us -> 86.9 us  [shards(): pl.pallas_call(functools.partial(kernel, planes), out_shape=(jax.ShapeDty...]
where the time goes in v2:
time: 92.8 us; the launch traced here: 92.6 us
  Pallas kernels  86.9 us (94%)
  local copies, waits for them, and re-layouts  4.46 us (5%)
  between operations  1.29 us (1%)
    pallas_call x1, Pallas kernels, shards(): pl.pallas_call(functools.partial(kernel, planes), out_shape=(jax.ShapeDty...  86.9 us
    unnamed x2, local copies, waits for them, and re-layouts  3.13 us

profile of v2, /device:TPU:1, one launch (start us, length us, event | category | flops | bytes accessed | tf_op | source)
XLA Modules:
  0.0 92.6 jit_solution(17021191547514253735)
XLA Ops:
  1.3 86.9 %shard_map.67 = (f32[16,2048]{1,0:T(8,128)}, f32[16,2048]{1,0:T(8,128)}, f32[16,128]{1,0:T(8,128)}) custom-call(s32[1]{0:T(128)S(6)} %copy.9.count_ref, bf16[512,2048]{1,0:T(8,128)(2,1)} %a_hbm.1, bf16[512,128]{1,0:T(8,128)(2,1)} %b_hbm.1, bf16[2048,2048]{1,0:T(8,128)(2,1)} %n_hbm.1), custom_call_target="tpu_custom_call" | custom-call | tf_op jit(solution)/shard_map/pallas_call | solution.py:426
  88.2 1.3 %slice_reduce_fusion = f32[16]{0:T(128)} fusion(f32[16,128]{1,0:T(8,128)} %get-tuple-element.8), kind=kLoop, calls=%fused_computation | loop fusion | bytes 128 | tf_op jit(solution)/shard_map/slice | solution.py:479
  89.5 1.6 %copy.10 = f32[2048,16]{0,1:T(8,128)} copy(f32[2048,16]{0,1:T(8,128)} %bitcast.3) | data formatting | bytes 262144
  91.1 1.6 %copy.11 = f32[2048,16]{0,1:T(8,128)} copy(f32[2048,16]{0,1:T(8,128)} %bitcast.2) | data formatting | bytes 262144

commit v3 on v2

--- a/solution.py
+++ b/solution.py
@@ -87,12 +87,8 @@
         )
 
     barrier = pltpu.get_barrier_semaphore()
-    partners = (
-        [partner]
-        + [on_chip(c) for c in plane_chips]
-        + [on_plane(k) for k in other_planes]
-        + [on_plane(k, True) for k in other_planes]
-    )
+    partners = [on_plane(k, other) for k in other_planes for other in (False, True)]
+    partners += [on_chip(c) for c in plane_chips] + [partner]
     for device in partners:
         pl.semaphore_signal(barrier, inc=1, device_id=device, device_id_type=MESH)
 
@@ -101,7 +97,6 @@
     load_n = pltpu.make_async_copy(n_hbm, n, load_sem.at[2])
     load_b.start()
     load_a.start()
-    load_n.start()
 
     ours = pl.ds(pl.multiple_of(core * half, half), half)
     theirs = pl.ds(pl.multiple_of((1 - core) * half, half), half)
@@ -203,6 +198,7 @@
     first_residue = shown * jnp.transpose(b[...].astype(jnp.float32))
     p0[pl.ds(0, columns)] = first_residue.astype(jnp.bfloat16)
     load_a.wait()
+    load_n.start()
 
     start_residue = p0[pl.ds(0, columns)]
     for j in range(width // TILE):
@@ -219,6 +215,22 @@
     mine = pl.ds(pl.multiple_of(lax.rem(z, per_core) * own_cols, own_cols), own_cols)
     spread = width // LANES
 
+    def recur(first):
+        u_own = ucol[pl.ds(pl.multiple_of(core * half, half) + lax.rem(z, per_core) * own_cols, own_cols)]
+        v_own = vcol[mine]
+        rho, phi, start = (scalars[core, pl.ds(k * own_cols, own_cols)] for k in range(3))
+        search = state[core, pl.ds(own_cols, own_cols)]
+        radius = jnp.sqrt(rho * rho + u_own * u_own)
+        cosine = rho / radius
+        sine = u_own / radius
+        state[core, pl.ds(0, own_cols)] = (
+            state[core, pl.ds(0, own_cols)] + wide(cosine * phi / radius, spread) * search
+        )
+        state[core, pl.ds(own_cols, own_cols)] = rv[mine] - wide(sine * v_own / radius, spread) * search
+        scalars[core, pl.ds(0, own_cols)] = jnp.where(first, v_own, -cosine * v_own)
+        scalars[core, pl.ds(own_cols, own_cols)] = jnp.where(first, u_own, sine * phi)
+        scalars[core, pl.ds(2 * own_cols, own_cols)] = jnp.where(first, u_own, start)
+
     def turn(i, carry):
         par = lax.rem(i, 2)
 
@@ -230,7 +242,6 @@
                 send_group(part[ours, lanes] + crecv[:, lanes].astype(jnp.float32), dy)
             residue_copy.wait_recv()
             pref[...] = jnp.concatenate([p0[ours], p0[pl.ds(columns, half)]], axis=1).astype(jnp.float32)
-            keep_squares()
 
         @pl.when(i > 0)
         def _():
@@ -239,7 +250,12 @@
                 lanes = pl.ds(pl.multiple_of(row_at(dy) * GROUP, GROUP), GROUP)
                 send_group(dot(residue, a[:, lanes]), dy)
 
+        keep_squares()
         squares_plane()
+
+        @pl.when(i > 0)
+        def _():
+            recur(i == 1)
 
         @pl.when(i == 0)
         def _():
@@ -340,23 +356,6 @@
         for c in plane_chips:
             plane_copy(c).wait_send()
             plane_sq(c).wait_send()
-        keep_squares()
-
-        first = i == 0
-        u_own = ucol[pl.ds(pl.multiple_of(core * half, half) + lax.rem(z, per_core) * own_cols, own_cols)]
-        v_own = vcol[mine]
-        rho, phi, start = (scalars[core, pl.ds(k * own_cols, own_cols)] for k in range(3))
-        search = state[core, pl.ds(own_cols, own_cols)]
-        radius = jnp.sqrt(rho * rho + u_own * u_own)
-        cosine = rho / radius
-        sine = u_own / radius
-        state[core, pl.ds(0, own_cols)] = (
-            state[core, pl.ds(0, own_cols)] + wide(cosine * phi / radius, spread) * search
-        )
-        state[core, pl.ds(own_cols, own_cols)] = rv[mine] - wide(sine * v_own / radius, spread) * search
-        scalars[core, pl.ds(0, own_cols)] = jnp.where(first, v_own, -cosine * v_own)
-        scalars[core, pl.ds(own_cols, own_cols)] = jnp.where(first, u_own, sine * phi)
-        scalars[core, pl.ds(2 * own_cols, own_cols)] = jnp.where(first, u_own, start)
 
         for k in other_planes:
             depth_copy(par, k).wait_send()
@@ -367,15 +366,17 @@
 
     lax.fori_loop(0, ITERS, turn, 0)
 
+    keep_squares()
     squares_plane()
-    state_copy.start()
-    scalars_copy.start()
+    recur(ITERS == 1)
     fsq[core, z] = squares_of_plane()
     last_core = remote(fsq.at[core, z], fsq.at[core, z], fsqs_sem.at[1 - core, z], fsqr_sem.at[core, z], partner)
     for k in other_planes:
         last_sq(k, False).start()
         last_sq(k, True).start()
     last_core.start()
+    state_copy.start()
+    scalars_copy.start()
 
     holder = lax.div(z, per_core)
     state_arrival.wait_recv()
@@ -414,6 +415,14 @@
     for k in other_planes:
         last_sq(k, False).wait_send()
         last_sq(k, True).wait_send()
+
+
+def finish(sol_in, coef_in, ratio_in, sol_ref, coef_ref, ratio_ref):
+    sol_ref[...] = sol_in[...]
+    coef_ref[...] = coef_in[...]
+    ratio = ratio_in[...]
+    square = jnp.concatenate([ratio] * (LANES // ratio.shape[0]), axis=0)
+    ratio_ref[...] = jnp.transpose(square)[0:1, : ratio.shape[0]]
 
 
 def shards(planes, matrix, right_side, precond, row_counts):
@@ -476,7 +485,15 @@
             collective_id=0, has_side_effects=True, vmem_limit_bytes=60 * 1024 * 1024
         ),
     )(row_counts, matrix, right_side, precond)
-    return solution.T, coeffs.T, ratio[:, 0]
+    solution, coeffs, ratio = pl.pallas_call(
+        finish,
+        out_shape=(
+            jax.ShapeDtypeStruct((own_cols, width), f32),
+            jax.ShapeDtypeStruct((own_cols, width), f32),
+            jax.ShapeDtypeStruct((1, own_cols), f32),
+        ),
+    )(solution, coeffs, ratio)
+    return solution.T, coeffs.T, ratio[0]
 
 
 def solution(mesh):

time: 92.8 us -> 88.9 us (0.958)
  local copies, waits for them, and re-layouts: 4.46 us -> 0 us
    unnamed x2 -> x0, local copies, waits for them, and re-layouts: 3.13 us -> none
    pallas_call x0 -> x1, Pallas kernels: none -> 1.68 us  [shards(): pl.pallas_call(finish, out_shape=(jax.ShapeDtypeStruct((own_cols, width),...]
    slice x1 -> x0, local copies, waits for them, and re-layouts: 1.32 us -> none  [shards(): return (solution.T, coeffs.T, ratio[:, 0])]
    pallas_call x1, Pallas kernels: 86.9 us -> 85.8 us  [shards(): pl.pallas_call(functools.partial(kernel, planes), out_shape=(jax.ShapeDty...]
where the time goes in v3:
time: 88.9 us; the launch traced here: 88.8 us
  Pallas kernels  87.5 us (98%)
  between operations  1.29 us (1%)
    pallas_call x1, Pallas kernels, shards(): pl.pallas_call(functools.partial(kernel, planes), out_shape=(jax.ShapeDty...  85.8 us

profile of v3, /device:TPU:1, one launch (start us, length us, event | category | flops | bytes accessed | tf_op | source)
XLA Modules:
  0.0 88.8 jit_solution(12038386716675968136)
XLA Ops:
  1.3 85.8 %shard_map.67 = (f32[16,2048]{1,0:T(8,128)}, f32[16,2048]{1,0:T(8,128)}, f32[16,128]{1,0:T(8,128)}) custom-call(s32[1]{0:T(128)S(6)} %copy.7.count_ref, bf16[512,2048]{1,0:T(8,128)(2,1)} %a_hbm.1, bf16[512,128]{1,0:T(8,128)(2,1)} %b_hbm.1, bf16[2048,2048]{1,0:T(8,128)(2,1)} %n_hbm.1), custom_call_target="tpu_custom_call" | custom-call | tf_op jit(solution)/shard_map/pallas_call | solution.py:435
  87.1 1.7 %shard_map.68 = (f32[16,2048]{1,0:T(8,128)}, f32[16,2048]{1,0:T(8,128)}, f32[1,16]{1,0:T(1,128)}) custom-call(f32[16,2048]{1,0:T(8,128)} %get-tuple-element.9.sol_in, f32[16,2048]{1,0:T(8,128)} %get-tuple-element.10.coef_in, f32[16,128]{1,0:T(8,128)} %get-tuple-element.11.ratio_in), custom_call_target="tpu_custom_call" | custom-call | tf_op jit(solution)/shard_map/pallas_call | solution.py:488

commit v4 on v3

--- a/solution.py
+++ b/solution.py
@@ -44,13 +44,13 @@
     planes,
     count_ref, a_hbm, b_hbm, n_hbm,
     sol_ref, coef_ref, ratio_ref,
-    a, at, b, n, nt, rv, raw, vb, pushed, pref, pb, p0, q, part, partb, crecv, xsend, xrecv, ownrow, zbuf,
-    live, csq, xsq, zsq, fsq, state, scalars, ucol, vcol,
+    a, b, n, bm, bt, raw, image, pref, pb, p0, q, part, partb, crecv, xsend, xrecv, ownrow, zbuf,
+    live, csq, xsq, zsq, fsq, state, scalars, ucol, vcol, vinv, sums,
     load_sem, cs_sem, cr_sem, ps_sem, pr_sem, ls_sem, lr_sem, as_sem, ar_sem,
     xs_sem, xr_sem, zs_sem, zr_sem, gs_sem, gr_sem,
     xsqs_sem, xsqr_sem, zsqs_sem, zsqr_sem, fsqs_sem, fsqr_sem, ts_sem, tr_sem, us_sem, ur_sem,
 ):
-    half, width = rv.shape
+    half, width = raw.shape
     columns = 2 * half
     rows = b.shape[0]
     both = 2 * rows
@@ -189,7 +189,8 @@
             if dy or dx:
                 plane_copy(chip_at(dy, dx)).start()
 
-    rv[...] = jnp.zeros_like(rv)
+    raw[...] = jnp.zeros_like(raw)
+    vinv[...] = jnp.zeros_like(vinv)
     state[...] = jnp.zeros_like(state)
     scalars[...] = jnp.zeros_like(scalars)
     shown = (lax.broadcasted_iota(jnp.int32, (1, rows), 1) < count_ref[0]).astype(jnp.float32)
@@ -226,10 +227,48 @@
         state[core, pl.ds(0, own_cols)] = (
             state[core, pl.ds(0, own_cols)] + wide(cosine * phi / radius, spread) * search
         )
-        state[core, pl.ds(own_cols, own_cols)] = rv[mine] - wide(sine * v_own / radius, spread) * search
+        state[core, pl.ds(own_cols, own_cols)] = raw[mine] * wide(vinv[mine], spread) - wide(sine * v_own / radius, spread) * search
         scalars[core, pl.ds(0, own_cols)] = jnp.where(first, v_own, -cosine * v_own)
         scalars[core, pl.ds(own_cols, own_cols)] = jnp.where(first, u_own, sine * phi)
         scalars[core, pl.ds(2 * own_cols, own_cols)] = jnp.where(first, u_own, start)
+
+    def group(dy):
+        return pl.ds(pl.multiple_of(row_at(dy) * GROUP, GROUP), GROUP)
+
+    def group_arrival(dy):
+        for dx in SEND_COLS:
+            if dy or dx:
+                gather_arrival(chip_at(dy, dx)).wait_recv()
+
+    def folded(value):
+        total = value[:, :LANES] * value[:, :LANES]
+        for k in range(1, value.shape[1] // LANES):
+            block = value[:, k * LANES : (k + 1) * LANES]
+            total = total + block * block
+        return total
+
+    def multiply(first):
+        lines = pl.ds(first, rows)
+
+        def step(k, c):
+            here = pl.ds(pl.multiple_of(k * 2 * TILE, 2 * TILE), 2 * TILE)
+            bm[lines, here] = dot(a[lines], n[:, here]).astype(jnp.bfloat16)
+            return c
+
+        lax.fori_loop(0, width // (2 * TILE), step, 0)
+
+    def flip():
+        lines = lax.broadcasted_iota(jnp.int32, (TILE, TILE), 0)
+        same = (lines == lax.broadcasted_iota(jnp.int32, (TILE, TILE), 1)).astype(jnp.bfloat16)
+
+        def step(k, c):
+            here = pl.ds(pl.multiple_of(k * TILE, TILE), TILE)
+            for j in range(width // TILE):
+                lanes = slice(j * TILE, (j + 1) * TILE)
+                bt[lanes, here] = dot_nt(same, bm[here, lanes]).astype(jnp.bfloat16)
+            return c
+
+        lax.fori_loop(0, both // TILE, step, 0)
 
     def turn(i, carry):
         par = lax.rem(i, 2)
@@ -248,7 +287,7 @@
             residue = pb[...]
             for dy in SEND_ROWS:
                 lanes = pl.ds(pl.multiple_of(row_at(dy) * GROUP, GROUP), GROUP)
-                send_group(dot(residue, a[:, lanes]), dy)
+                send_group(dot(residue, bm[:, lanes]), dy)
 
         keep_squares()
         squares_plane()
@@ -259,18 +298,8 @@
 
         @pl.when(i == 0)
         def _():
-            lines = lax.broadcasted_iota(jnp.int32, (TILE, TILE), 0)
-            same = (lines == lax.broadcasted_iota(jnp.int32, (TILE, TILE), 1)).astype(jnp.bfloat16)
             load_n.wait()
-
-            def flip_n(k, c):
-                here = pl.ds(pl.multiple_of(k * TILE, TILE), TILE)
-                for j in range(width // TILE):
-                    lanes = slice(j * TILE, (j + 1) * TILE)
-                    nt[lanes, here] = dot_nt(same, n[here, lanes]).astype(jnp.bfloat16)
-                return c
-
-            lax.fori_loop(0, width // TILE, flip_n, 0)
+            multiply(0)
 
         own = ownrow[x]
         for c in plane_chips:
@@ -284,19 +313,9 @@
 
         @pl.when(i == 0)
         def _():
-            lines = lax.broadcasted_iota(jnp.int32, (TILE, TILE), 0)
-            same = (lines == lax.broadcasted_iota(jnp.int32, (TILE, TILE), 1)).astype(jnp.bfloat16)
             a_copy.wait_recv()
             live_copy.wait_recv()
-
-            def flip_a(k, c):
-                here = pl.ds(pl.multiple_of(k * TILE, TILE), TILE)
-                for j in range(width // TILE):
-                    lanes = slice(j * TILE, (j + 1) * TILE)
-                    at[lanes, here] = dot_nt(same, a[here, lanes]).astype(jnp.bfloat16)
-                return c
-
-            lax.fori_loop(0, both // TILE, flip_a, 0)
+            multiply(rows)
 
         for k in other_planes:
             depth_sq_arrival(par, k).wait_recv()
@@ -314,42 +333,50 @@
 
         for c in plane_chips:
             gather_copy(c).start()
-        u_tile = wide(u, TILE // LANES)
-        squares = jnp.zeros((half, LANES), jnp.float32)
-        for turn_at, dy in enumerate(TAKE_ROWS):
-            for dx in SEND_COLS:
-                if dy or dx:
-                    gather_arrival(chip_at(dy, dx)).wait_recv()
-            here = pl.ds(pl.multiple_of(row_at(dy) * GROUP, GROUP), GROUP)
-            taken = q[:, here]
-            for j in range(width // TILE):
-                lanes = slice(j * TILE, (j + 1) * TILE)
-                before = raw[:, lanes] if turn_at else -u_tile * rv[:, lanes]
-                value = before + dot(taken, n[here, lanes])
-                raw[:, lanes] = value
-                if turn_at == SIDE - 1:
-                    for s in range(TILE // LANES):
-                        block = value[:, s * LANES : (s + 1) * LANES]
-                        squares = squares + block * block
-        v = jnp.sqrt(jnp.sum(squares, axis=1, keepdims=True) + FLOOR_SQ)
+
+        @pl.when(i == 0)
+        def _():
+            flip()
+            squares = jnp.zeros((half, LANES), jnp.float32)
+            for taken, dy in enumerate(TAKE_ROWS):
+                group_arrival(dy)
+                here = group(dy)
+                value = q[:, here]
+                for j in range(width // TILE):
+                    lanes = slice(j * TILE, (j + 1) * TILE)
+                    product = dot(value, n[here, lanes])
+                    if taken:
+                        product = raw[:, lanes] + product
+                    raw[:, lanes] = product
+                    if taken == SIDE - 1:
+                        squares = squares + folded(product)
+            sums[...] = squares
+            image[...] = dot(raw[...].astype(jnp.bfloat16), bt[...])
+
+        @pl.when(i > 0)
+        def _():
+            back = wide(u * vinv[...], SIDE)
+            squares = jnp.zeros((half, LANES), jnp.float32)
+            for taken, dy in enumerate(TAKE_ROWS):
+                group_arrival(dy)
+                here = group(dy)
+                value = q[:, here].astype(jnp.float32) - back * raw[:, here]
+                raw[:, here] = value
+                product = dot(value.astype(jnp.bfloat16), bt[here, :])
+                image[...] = image[...] + product if taken else product
+                squares = squares + folded(value)
+            sums[...] = squares
+
+        v = jnp.sqrt(jnp.sum(sums[...], axis=1, keepdims=True) + FLOOR_SQ)
         v = jnp.broadcast_to(v, (half, LANES))
+        inverse = 1.0 / v
         vcol[...] = v
-        inverse = wide(1.0 / v, TILE // LANES)
-        for j in range(width // TILE):
-            lanes = slice(j * TILE, (j + 1) * TILE)
-            unit = raw[:, lanes] * inverse
-            rv[:, lanes] = unit
-            vb[:, lanes] = unit.astype(jnp.bfloat16)
-
-        unit = vb[...]
-        for j in range(width // TILE):
-            lanes = slice(j * TILE, (j + 1) * TILE)
-            pushed[:, lanes] = dot(unit, nt[:, lanes]).astype(jnp.bfloat16)
-        front = pushed[...]
-        back = wide(v / u, rows // LANES)
+        vinv[...] = inverse
+
+        scale, back = wide(inverse, rows // LANES), wide(v / u, rows // LANES)
         for h in range(2):
             lanes = slice(h * rows, (h + 1) * rows)
-            residue = live[h] * (dot(front, at[:, lanes]) - back * pref[:, lanes])
+            residue = live[h] * (scale * image[:, lanes] - back * pref[:, lanes])
             pref[:, lanes] = residue
             pb[:, lanes] = residue.astype(jnp.bfloat16)
 
@@ -385,7 +412,7 @@
     stacked = jnp.concatenate([high, low], axis=0)
     for j in range(width // TILE):
         lanes = slice(j * TILE, (j + 1) * TILE)
-        product = dot(stacked, nt[:, lanes])
+        product = dot_nt(stacked, n[lanes, :])
         raw[pl.ds(0, 2 * own_cols), lanes] = product[: 2 * own_cols] + product[2 * own_cols :]
 
     last_sq_arrival(1 - core, z).wait_recv()
@@ -443,14 +470,12 @@
         out_specs=(pl.BlockSpec(memory_space=vmem),) * 3,
         scratch_shapes=[
             vmem((2 * rows, width), bf16),
-            vmem((width, 2 * rows), bf16),
             vmem((rows, columns), bf16),
             vmem((width, width), bf16),
-            vmem((width, width), bf16),
+            vmem((2 * rows, width), bf16),
+            vmem((width, 2 * rows), bf16),
             vmem((half, width), f32),
-            vmem((half, width), f32),
-            vmem((half, width), bf16),
-            vmem((half, width), bf16),
+            vmem((half, 2 * rows), f32),
             vmem((half, 2 * rows), f32),
             vmem((half, 2 * rows), bf16),
             vmem((columns + half, rows), bf16),
@@ -470,6 +495,8 @@
             vmem((2, 2 * own_cols, width), f32),
             vmem((2, 3 * own_cols, LANES), f32),
             vmem((columns, LANES), f32),
+            vmem((half, LANES), f32),
+            vmem((half, LANES), f32),
             vmem((half, LANES), f32),
             dma((3,)),
             dma, dma, dma, dma, dma, dma, dma, dma,

time: 88.9 us -> 82.3 us (0.926)
  Pallas kernels: 87.5 us -> 80.8 us
    pallas_call x1, Pallas kernels: 85.8 us -> 79.1 us  [shards(): pl.pallas_call(functools.partial(kernel, planes), out_shape=(jax.ShapeDty...]
where the time goes in v4:
time: 82.3 us; the launch traced here: 82.1 us
  Pallas kernels  80.8 us (98%)
  between operations  1.29 us (2%)
    pallas_call x1, Pallas kernels, shards(): pl.pallas_call(functools.partial(kernel, planes), out_shape=(jax.ShapeDty...  79.1 us
    pallas_call x1, Pallas kernels, shards(): pl.pallas_call(finish, out_shape=(jax.ShapeDtypeStruct((own_cols, width),...  1.68 us

profile of v4, /device:TPU:1, one launch (start us, length us, event | category | flops | bytes accessed | tf_op | source)
XLA Modules:
  0.0 82.1 jit_solution(12075666859048588424)
XLA Ops:
  1.3 79.1 %shard_map.67 = (f32[16,2048]{1,0:T(8,128)}, f32[16,2048]{1,0:T(8,128)}, f32[16,128]{1,0:T(8,128)}) custom-call(s32[1]{0:T(128)S(6)} %copy.7.count_ref, bf16[512,2048]{1,0:T(8,128)(2,1)} %a_hbm.1, bf16[512,128]{1,0:T(8,128)(2,1)} %b_hbm.1, bf16[2048,2048]{1,0:T(8,128)(2,1)} %n_hbm.1), custom_call_target="tpu_custom_call" | custom-call | tf_op jit(solution)/shard_map/pallas_call | solution.py:462
  80.4 1.7 %shard_map.68 = (f32[16,2048]{1,0:T(8,128)}, f32[16,2048]{1,0:T(8,128)}, f32[1,16]{1,0:T(1,128)}) custom-call(f32[16,2048]{1,0:T(8,128)} %get-tuple-element.9.sol_in, f32[16,2048]{1,0:T(8,128)} %get-tuple-element.10.coef_in, f32[16,128]{1,0:T(8,128)} %get-tuple-element.11.ratio_in), custom_call_target="tpu_custom_call" | custom-call | tf_op jit(solution)/shard_map/pallas_call | solution.py:515

commit v5 on v4

--- a/solution.py
+++ b/solution.py
@@ -14,6 +14,7 @@
 CHIPS = SIDE * SIDE
 LANES = 128
 TILE = 256
+PARTS = 1
 GROUP = SIDE * LANES
 
 SEND_ROWS = (2, 1, 3, 0)
@@ -42,9 +43,9 @@
 
 def kernel(
     planes,
-    count_ref, a_hbm, b_hbm, n_hbm,
+    count_hbm, a_hbm, b_hbm, n_hbm,
     sol_ref, coef_ref, ratio_ref,
-    a, b, n, bm, bt, raw, image, pref, pb, p0, q, part, partb, crecv, xsend, xrecv, ownrow, zbuf,
+    count, a, b, n, bm, bt, raw, image, pref, pb, p0, q, part, partb, crecv, xsend, xrecv, ownrow, zbuf,
     live, csq, xsq, zsq, fsq, state, scalars, ucol, vcol, vinv, sums,
     load_sem, cs_sem, cr_sem, ps_sem, pr_sem, ls_sem, lr_sem, as_sem, ar_sem,
     xs_sem, xr_sem, zs_sem, zr_sem, gs_sem, gr_sem,
@@ -95,6 +96,8 @@
     load_b = pltpu.make_async_copy(b_hbm, b, load_sem.at[0])
     load_a = pltpu.make_async_copy(a_hbm, a.at[pl.ds(0, rows)], load_sem.at[1])
     load_n = pltpu.make_async_copy(n_hbm, n, load_sem.at[2])
+    load_count = pltpu.make_async_copy(count_hbm, count, load_sem.at[3])
+    load_count.start()
     load_b.start()
     load_a.start()
 
@@ -102,7 +105,12 @@
     theirs = pl.ds(pl.multiple_of((1 - core) * half, half), half)
     ones = jnp.ones((8, both), jnp.bfloat16)
 
-    core_copy = remote(partb.at[theirs], crecv, cs_sem, cr_sem, partner)
+    def group(dy):
+        return pl.ds(pl.multiple_of(row_at(dy) * GROUP, GROUP), GROUP)
+
+    def core_copy(dy):
+        return remote(partb.at[theirs, group(dy)], crecv.at[:, group(dy)], cs_sem.at[dy], cr_sem.at[dy], partner)
+
     residue_copy = remote(p0.at[theirs], p0.at[pl.ds(columns, half)], ps_sem, pr_sem, partner)
     live_copy = remote(live.at[0], live.at[1], ls_sem, lr_sem, partner)
     a_copy = remote(a.at[pl.ds(0, rows)], a.at[pl.ds(rows, rows)], as_sem, ar_sem, partner)
@@ -111,11 +119,18 @@
     scalars_copy = remote(scalars.at[core], scalars.at[core], us_sem, ur_sem, partner)
     scalars_arrival = remote(scalars.at[1 - core], scalars.at[1 - core], us_sem, ur_sem, partner)
 
-    def plane_copy(c):
-        return remote(xsend.at[c], xrecv.at[chip], xs_sem.at[c], xr_sem.at[chip], on_chip(c))
-
-    def plane_arrival(c):
-        return remote(xsend.at[c], xrecv.at[c], xs_sem.at[c], xr_sem.at[c], on_chip(c))
+    part_rows = half // PARTS
+
+    def part_of(g):
+        return pl.ds(g * part_rows, part_rows)
+
+    def plane_copy(c, g):
+        mine_at, there = xsend.at[c, part_of(g)], xrecv.at[chip, part_of(g)]
+        return remote(mine_at, there, xs_sem.at[c, g], xr_sem.at[chip, g], on_chip(c))
+
+    def plane_arrival(c, g):
+        mine_at, here = xsend.at[c, part_of(g)], xrecv.at[c, part_of(g)]
+        return remote(mine_at, here, xs_sem.at[c, g], xr_sem.at[c, g], on_chip(c))
 
     def plane_sq(c):
         return remote(xsq.at[chip], xsq.at[chip], xsqs_sem.at[c], xsqr_sem.at[chip], on_chip(c))
@@ -123,11 +138,13 @@
     def plane_sq_arrival(c):
         return remote(xsq.at[c], xsq.at[c], xsqs_sem.at[c], xsqr_sem.at[c], on_chip(c))
 
-    def depth_copy(par, k):
-        return remote(zbuf.at[par, z], zbuf.at[par, z], zs_sem.at[par, k], zr_sem.at[par, z], on_plane(k))
-
-    def depth_arrival(par, k):
-        return remote(zbuf.at[par, k], zbuf.at[par, k], zs_sem.at[par, k], zr_sem.at[par, k], on_plane(k))
+    def depth_copy(par, k, g):
+        block = zbuf.at[par, z, part_of(g)]
+        return remote(block, block, zs_sem.at[par, k, g], zr_sem.at[par, z, g], on_plane(k))
+
+    def depth_arrival(par, k, g):
+        block = zbuf.at[par, k, part_of(g)]
+        return remote(block, block, zs_sem.at[par, k, g], zr_sem.at[par, k, g], on_plane(k))
 
     def depth_sq(par, k):
         return remote(zsq.at[par, z], zsq.at[par, z], zsqs_sem.at[par, k], zsqr_sem.at[par, z], on_plane(k))
@@ -142,14 +159,14 @@
     def last_sq_arrival(h, k):
         return remote(fsq.at[h, k], fsq.at[h, k], fsqs_sem.at[h, k], fsqr_sem.at[h, k], partner)
 
-    def piece(c):
-        return q.at[:, pl.ds(pl.multiple_of(c * LANES, LANES), LANES)]
-
-    def gather_copy(c):
-        return remote(piece(chip), piece(chip), gs_sem.at[c], gr_sem.at[chip], on_chip(c))
-
-    def gather_arrival(c):
-        return remote(piece(c), piece(c), gs_sem.at[c], gr_sem.at[c], on_chip(c))
+    def piece(c, g):
+        return q.at[part_of(g), pl.ds(pl.multiple_of(c * LANES, LANES), LANES)]
+
+    def gather_copy(c, g):
+        return remote(piece(chip, g), piece(chip, g), gs_sem.at[c, g], gr_sem.at[chip, g], on_chip(c))
+
+    def gather_arrival(c, g):
+        return remote(piece(c, g), piece(c, g), gs_sem.at[c, g], gr_sem.at[c, g], on_chip(c))
 
     def keep_squares():
         square = pref[...] * pref[...]
@@ -187,13 +204,14 @@
                 ownrow[s] = block
         for dx in SEND_COLS:
             if dy or dx:
-                plane_copy(chip_at(dy, dx)).start()
+                plane_copy(chip_at(dy, dx), 0).start()
 
     raw[...] = jnp.zeros_like(raw)
     vinv[...] = jnp.zeros_like(vinv)
     state[...] = jnp.zeros_like(state)
     scalars[...] = jnp.zeros_like(scalars)
-    shown = (lax.broadcasted_iota(jnp.int32, (1, rows), 1) < count_ref[0]).astype(jnp.float32)
+    load_count.wait()
+    shown = (lax.broadcasted_iota(jnp.int32, (1, rows), 1) < count[0]).astype(jnp.float32)
     live[0] = shown
     load_b.wait()
     first_residue = shown * jnp.transpose(b[...].astype(jnp.float32))
@@ -208,7 +226,8 @@
         part[:, lanes] = product
         partb[:, lanes] = product.astype(jnp.bfloat16)
     pl.semaphore_wait(barrier, len(partners))
-    core_copy.start()
+    for dy in SEND_ROWS:
+        core_copy(dy).start()
     residue_copy.start()
     live_copy.start()
     a_copy.start()
@@ -232,13 +251,11 @@
         scalars[core, pl.ds(own_cols, own_cols)] = jnp.where(first, u_own, sine * phi)
         scalars[core, pl.ds(2 * own_cols, own_cols)] = jnp.where(first, u_own, start)
 
-    def group(dy):
-        return pl.ds(pl.multiple_of(row_at(dy) * GROUP, GROUP), GROUP)
-
     def group_arrival(dy):
         for dx in SEND_COLS:
             if dy or dx:
-                gather_arrival(chip_at(dy, dx)).wait_recv()
+                for g in range(PARTS):
+                    gather_arrival(chip_at(dy, dx), g).wait_recv()
 
     def folded(value):
         total = value[:, :LANES] * value[:, :LANES]
@@ -275,8 +292,8 @@
 
         @pl.when(i == 0)
         def _():
-            core_copy.wait_recv()
             for dy in SEND_ROWS:
+                core_copy(dy).wait_recv()
                 lanes = pl.ds(pl.multiple_of(row_at(dy) * GROUP, GROUP), GROUP)
                 send_group(part[ours, lanes] + crecv[:, lanes].astype(jnp.float32), dy)
             residue_copy.wait_recv()
@@ -289,6 +306,9 @@
                 lanes = pl.ds(pl.multiple_of(row_at(dy) * GROUP, GROUP), GROUP)
                 send_group(dot(residue, bm[:, lanes]), dy)
 
+        for g in range(1, PARTS):
+            for c in plane_chips:
+                plane_copy(c, g).start()
         keep_squares()
         squares_plane()
 
@@ -301,14 +321,16 @@
             load_n.wait()
             multiply(0)
 
-        own = ownrow[x]
-        for c in plane_chips:
-            plane_arrival(c).wait_recv()
-            own = own + xrecv[c].astype(jnp.float32)
-        zbuf[par, z] = own.astype(jnp.bfloat16)
+        for g in range(PARTS):
+            own = ownrow[x, part_of(g)]
+            for c in plane_chips:
+                plane_arrival(c, g).wait_recv()
+                own = own + xrecv[c, part_of(g)].astype(jnp.float32)
+            zbuf[par, z, part_of(g)] = own.astype(jnp.bfloat16)
+            for k in other_planes:
+                depth_copy(par, k, g).start()
         zsq[par, z] = squares_of_plane()
         for k in other_planes:
-            depth_copy(par, k).start()
             depth_sq(par, k).start()
 
         @pl.when(i == 0)
@@ -317,6 +339,16 @@
             live_copy.wait_recv()
             multiply(rows)
 
+        for g in range(PARTS):
+            for k in other_planes:
+                depth_arrival(par, k, g).wait_recv()
+            total = zbuf[par, 0, part_of(g)].astype(jnp.float32)
+            for k in range(1, planes):
+                total = total + zbuf[par, k, part_of(g)].astype(jnp.float32)
+            q[part_of(g), pl.ds(pl.multiple_of(chip * LANES, LANES), LANES)] = total.astype(jnp.bfloat16)
+
+            for c in plane_chips:
+                gather_copy(c, g).start()
         for k in other_planes:
             depth_sq_arrival(par, k).wait_recv()
         total = zsq[par, 0]
@@ -324,15 +356,7 @@
             total = total + zsq[par, k]
         keep_norm(total)
         u = ucol[ours]
-        for k in other_planes:
-            depth_arrival(par, k).wait_recv()
-        total = zbuf[par, 0].astype(jnp.float32)
-        for k in range(1, planes):
-            total = total + zbuf[par, k].astype(jnp.float32)
-        q[:, pl.ds(pl.multiple_of(chip * LANES, LANES), LANES)] = (total / u).astype(jnp.bfloat16)
-
-        for c in plane_chips:
-            gather_copy(c).start()
+        shrink = 1.0 / u
 
         @pl.when(i == 0)
         def _():
@@ -347,6 +371,8 @@
                     product = dot(value, n[here, lanes])
                     if taken:
                         product = raw[:, lanes] + product
+                    if taken == SIDE - 1:
+                        product = product * wide(shrink, TILE // LANES)
                     raw[:, lanes] = product
                     if taken == SIDE - 1:
                         squares = squares + folded(product)
@@ -360,7 +386,7 @@
             for taken, dy in enumerate(TAKE_ROWS):
                 group_arrival(dy)
                 here = group(dy)
-                value = q[:, here].astype(jnp.float32) - back * raw[:, here]
+                value = wide(shrink, SIDE) * q[:, here].astype(jnp.float32) - back * raw[:, here]
                 raw[:, here] = value
                 product = dot(value.astype(jnp.bfloat16), bt[here, :])
                 image[...] = image[...] + product if taken else product
@@ -381,14 +407,17 @@
             pb[:, lanes] = residue.astype(jnp.bfloat16)
 
         for c in plane_chips:
-            plane_copy(c).wait_send()
+            for g in range(PARTS):
+                plane_copy(c, g).wait_send()
             plane_sq(c).wait_send()
 
         for k in other_planes:
-            depth_copy(par, k).wait_send()
+            for g in range(PARTS):
+                depth_copy(par, k, g).wait_send()
             depth_sq(par, k).wait_send()
         for c in plane_chips:
-            gather_copy(c).wait_send()
+            for g in range(PARTS):
+                gather_copy(c, g).wait_send()
         return carry
 
     lax.fori_loop(0, ITERS, turn, 0)
@@ -435,7 +464,9 @@
     sol_ref[...] = raw[pl.ds(0, own_cols)] + step * raw[pl.ds(own_cols, own_cols)]
     ratio_ref[...] = sine * phi / start
 
-    for copy in (core_copy, residue_copy, live_copy, a_copy, state_copy, scalars_copy, last_core):
+    for dy in SEND_ROWS:
+        core_copy(dy).wait_send()
+    for copy in (residue_copy, live_copy, a_copy, state_copy, scalars_copy, last_core):
         copy.wait_send()
     for c in plane_chips:
         plane_sq(c).wait_send()
@@ -466,9 +497,10 @@
             jax.ShapeDtypeStruct((own_cols, width), f32),
             jax.ShapeDtypeStruct((own_cols, LANES), f32),
         ),
-        in_specs=[pl.BlockSpec(memory_space=pltpu.SMEM)] + [pl.BlockSpec(memory_space=pl.ANY)] * 3,
+        in_specs=[pl.BlockSpec(memory_space=pl.ANY)] * 4,
         out_specs=(pl.BlockSpec(memory_space=vmem),) * 3,
         scratch_shapes=[
+            pltpu.SMEM((1,), jnp.int32),
             vmem((2 * rows, width), bf16),
             vmem((rows, columns), bf16),
             vmem((width, width), bf16),
@@ -498,11 +530,11 @@
             vmem((half, LANES), f32),
             vmem((half, LANES), f32),
             vmem((half, LANES), f32),
-            dma((3,)),
-            dma, dma, dma, dma, dma, dma, dma, dma,
-            dma((CHIPS,)), dma((CHIPS,)),
-            dma((2, planes)), dma((2, planes)),
-            dma((CHIPS,)), dma((CHIPS,)),
+            dma((4,)),
+            dma((SIDE,)), dma((SIDE,)), dma, dma, dma, dma, dma, dma,
+            dma((CHIPS, PARTS)), dma((CHIPS, PARTS)),
+            dma((2, planes, PARTS)), dma((2, planes, PARTS)),
+            dma((CHIPS, PARTS)), dma((CHIPS, PARTS)),
             dma((CHIPS,)), dma((CHIPS,)),
             dma((2, planes)), dma((2, planes)),
             dma((2, planes)), dma((2, planes)),

time: 82.3 us -> 79.8 us (0.970)
  Pallas kernels: 80.8 us -> 78.3 us
    pallas_call x1, Pallas kernels: 79.1 us -> 76.7 us  [shards(): pl.pallas_call(functools.partial(kernel, planes), out_shape=(jax.ShapeDty...]
where the time goes in v5:
time: 79.8 us; the launch traced here: 79.6 us
  Pallas kernels  78.3 us (98%)
  between operations  1.29 us (2%)
    pallas_call x1, Pallas kernels, shards(): pl.pallas_call(functools.partial(kernel, planes), out_shape=(jax.ShapeDty...  76.7 us
    pallas_call x1, Pallas kernels, shards(): pl.pallas_call(finish, out_shape=(jax.ShapeDtypeStruct((own_cols, width),...  1.68 us

profile of v5, /device:TPU:1, one launch (start us, length us, event | category | flops | bytes accessed | tf_op | source)
XLA Modules:
  0.0 79.6 jit_solution(11014535771511338492)
XLA Ops:
  1.3 76.7 %shard_map.67 = (f32[16,2048]{1,0:T(8,128)}, f32[16,2048]{1,0:T(8,128)}, f32[16,128]{1,0:T(8,128)}) custom-call(s32[1]{0:T(128)S(6)} %copy.7.count_hbm, bf16[512,2048]{1,0:T(8,128)(2,1)} %a_hbm.1, bf16[512,128]{1,0:T(8,128)(2,1)} %b_hbm.1, bf16[2048,2048]{1,0:T(8,128)(2,1)} %n_hbm.1), custom_call_target="tpu_custom_call" | custom-call | tf_op jit(solution)/shard_map/pallas_call | solution.py:493
  77.9 1.7 %shard_map.68 = (f32[16,2048]{1,0:T(8,128)}, f32[16,2048]{1,0:T(8,128)}, f32[1,16]{1,0:T(1,128)}) custom-call(f32[16,2048]{1,0:T(8,128)} %get-tuple-element.9.sol_in, f32[16,2048]{1,0:T(8,128)} %get-tuple-element.10.coef_in, f32[16,128]{1,0:T(8,128)} %get-tuple-element.11.ratio_in), custom_call_target="tpu_custom_call" | custom-call | tf_op jit(solution)/shard_map/pallas_call | solution.py:547

commit v6 on v5

--- a/solution.py
+++ b/solution.py
@@ -357,6 +357,14 @@
         keep_norm(total)
         u = ucol[ours]
         shrink = 1.0 / u
+        for c in plane_chips:
+            for g in range(PARTS):
+                plane_copy(c, g).wait_send()
+            plane_sq(c).wait_send()
+        for k in other_planes:
+            for g in range(PARTS):
+                depth_copy(par, k, g).wait_send()
+            depth_sq(par, k).wait_send()
 
         @pl.when(i == 0)
         def _():
@@ -406,15 +414,6 @@
             pref[:, lanes] = residue
             pb[:, lanes] = residue.astype(jnp.bfloat16)
 
-        for c in plane_chips:
-            for g in range(PARTS):
-                plane_copy(c, g).wait_send()
-            plane_sq(c).wait_send()
-
-        for k in other_planes:
-            for g in range(PARTS):
-                depth_copy(par, k, g).wait_send()
-            depth_sq(par, k).wait_send()
         for c in plane_chips:
             for g in range(PARTS):
                 gather_copy(c, g).wait_send()

time: 79.8 us -> 79.5 us (level)
  no operation moved by 1% of the time
where the time goes in v6:
time: 79.5 us; the launch traced here: 79.3 us
  Pallas kernels  78.1 us (98%)
  between operations  1.29 us (2%)
    pallas_call x1, Pallas kernels, shards(): pl.pallas_call(functools.partial(kernel, planes), out_shape=(jax.ShapeDty...  76.4 us
    pallas_call x1, Pallas kernels, shards(): pl.pallas_call(finish, out_shape=(jax.ShapeDtypeStruct((own_cols, width),...  1.68 us

profile of v6, /device:TPU:1, one launch (start us, length us, event | category | flops | bytes accessed | tf_op | source)
XLA Modules:
  0.0 79.3 jit_solution(14096360375203370611)
XLA Ops:
  1.3 76.4 %shard_map.67 = (f32[16,2048]{1,0:T(8,128)}, f32[16,2048]{1,0:T(8,128)}, f32[16,128]{1,0:T(8,128)}) custom-call(s32[1]{0:T(128)S(6)} %copy.7.count_hbm, bf16[512,2048]{1,0:T(8,128)(2,1)} %a_hbm.1, bf16[512,128]{1,0:T(8,128)(2,1)} %b_hbm.1, bf16[2048,2048]{1,0:T(8,128)(2,1)} %n_hbm.1), custom_call_target="tpu_custom_call" | custom-call | tf_op jit(solution)/shard_map/pallas_call | solution.py:492
  77.7 1.7 %shard_map.68 = (f32[16,2048]{1,0:T(8,128)}, f32[16,2048]{1,0:T(8,128)}, f32[1,16]{1,0:T(1,128)}) custom-call(f32[16,2048]{1,0:T(8,128)} %get-tuple-element.9.sol_in, f32[16,2048]{1,0:T(8,128)} %get-tuple-element.10.coef_in, f32[16,128]{1,0:T(8,128)} %get-tuple-element.11.ratio_in), custom_call_target="tpu_custom_call" | custom-call | tf_op jit(solution)/shard_map/pallas_call | solution.py:546
